TPU v7x, 32 devices: a whole 2x2x4 slice. The times are simulated.
32 devices in a mesh: pass: 8 (over z, x), cell: 4 (over y, core).
Axes of the slice: x: 2, y: 2, z: 4, core: 2. Of those that a mesh axis runs over, the one named last changes fastest.
Arguments:
- flow_state: float32 [2048, 4096], P('pass', 'cell'), may hold values from -6 to 6
- face_weights: float32 [4, 2048, 4096], P(None, 'pass', 'cell'), may hold values from 0.02 to 0.24
- forcing: float32 [2048, 4096], P('pass', 'cell'), may hold values from -1.2 to 1.2
- lagged_planes: float32 [8, 8, 4096], P('pass', None, 'cell'), may hold values from -6 to 6
- phase_lag: int32 [4, 2], replicated, may hold values from 0 to 8
- face_map: int32 [8, 4096], P('pass', 'cell'), may hold values from 0 to 4095, as said below
- surface_record: bfloat16 [8, 120, 4096], P('pass', None, 'cell'), may hold values from -6 to 6
- face_radius: float32 [2, 4096], P(None, 'cell'), may hold values from 0.3 to 1
- face_angle: float32 [2, 4096], P(None, 'cell'), may hold values from -0.3 to 0.3
- face_axial: float32 [2, 4096], P(None, 'cell'), may hold values from -0.3 to 0.3
- face_stagger: float32 [2, 4096], P(None, 'cell'), may hold values from -1.2 to 1.2
- face_area: float32 [2, 4096], P(None, 'cell'), may hold values from 0.5 to 1.5
- listeners: float32 [3, 1024], replicated, as said below
- observer_group: int32 [1024], replicated, may hold values from 0 to 15
Outputs:
- final_field: float32 [2048, 4096], P('pass', 'cell')
- acoustic: float32 [1024, 128], P('cell')
- array_signal: float32 [16, 128], replicated
Inputs may be any that keep to these rules, and one draw needn't show every extreme that they name: face_map[j, a] lies in the aligned block of 1024 axial indices that holds a, and for each j the entries of a block are a permutation of that block. `listeners`: every observer is between 1.3 and 4 from the anchor.
All inputs are finite; a program needn't handle non-finite values.
Results may differ from a plain program's by a relative error of at most 0.0035.
Values sent between devices are 32-bit elements; how exact they have to be, the bound alone decides.
A program may use at most 64 MiB of HBM per device.

v0:
```python
import math
import jax
import jax.numpy as jnp
from jax import lax
from jax.sharding import PartitionSpec as P

STEPS = 8
GROUPS = 16
sound_speed = 2.0


def padded(shard, sides, width):
    for axis, dim in sides:
        devices, length = (lax.axis_size(axis), shard.shape[dim])
        up = [(i, (i + 1) % devices) for i in range(devices - 1)]
        down = [(j, i) for i, j in up]
        last = lax.slice_in_dim(shard, length - width, length, axis=dim)
        initial = lax.slice_in_dim(shard, 0, width, axis=dim)
        before = lax.ppermute(last, axis, up)
        after = lax.ppermute(initial, axis, down)
        shard = jnp.concatenate([before, shard, after], axis=dim)
    return shard


def shifted(block, axis, distance):
    devices = range(lax.axis_size(axis))
    route = [((i - distance) % len(devices), i) for i in devices]
    return lax.ppermute(block, axis, route)


def relax(field, coeff, forcing, ghost_low, ghost_high):
    edges = jnp.stack([field[:, 0], field[:, -1]], axis=0)
    rim = padded(edges, (("cell", 0),), 1)
    below = jnp.concatenate([ghost_low[None, :], field[:-1, :]], axis=0)
    above = jnp.concatenate([field[1:, :], ghost_high[None, :]], axis=0)
    left = jnp.concatenate([rim[0][:, None], field[:, :-1]], axis=1)
    right = jnp.concatenate([field[:, 1:], rim[3][:, None]], axis=1)
    keep = 1.0 - coeff[0] - coeff[1] - coeff[2] - coeff[3]
    return (
        keep * field
        + coeff[0] * below
        + coeff[1] * above
        + coeff[2] * left
        + coeff[3] * right
        + forcing
    )


def time_rate(signal, axis):
    values = signal.astype(jnp.float32)
    length = values.shape[axis]
    inner = (
        lax.slice_in_dim(values, 2, length, axis=axis)
        - lax.slice_in_dim(values, 0, length - 2, axis=axis)
    ) * 0.5
    head = lax.slice_in_dim(values, 1, 2, axis=axis) - lax.slice_in_dim(values, 0, 1, axis=axis)
    tail = lax.slice_in_dim(values, length - 1, length, axis=axis) - lax.slice_in_dim(
        values, length - 2, length - 1, axis=axis
    )
    return jnp.concatenate([head, inner, tail], axis=axis).astype(jnp.bfloat16)


def kernel_pair(points, theta, radius, angle, axial, stagger, area, scale):
    phase = theta + angle
    cos_phase = jnp.cos(phase)
    sin_phase = jnp.sin(phase)
    normal_x = -jnp.cos(stagger) * sin_phase
    normal_y = jnp.cos(stagger) * cos_phase
    normal_z = jnp.sin(stagger)
    delta_x = points[0][:, None] - (radius * cos_phase)[None, :]
    delta_y = points[1][:, None] - (radius * sin_phase)[None, :]
    delta_z = points[2][:, None] - axial[None, :]
    dist_sq = delta_x * delta_x + delta_y * delta_y + delta_z * delta_z
    dist = jnp.sqrt(dist_sq)
    cosine = (
        normal_x[None, :] * delta_x + normal_y[None, :] * delta_y + normal_z[None, :] * delta_z
    ) / dist
    weight = (area * scale / (4.0 * math.pi))[None, :] * cosine
    press = (weight / dist_sq).astype(jnp.bfloat16)
    change = (weight / (sound_speed * dist)).astype(jnp.bfloat16)
    return jnp.concatenate([press, change], axis=1)


def on_device(
    flow_state,
    face_weights,
    forcing,
    lagged_planes,
    phase_lag,
    face_map,
    surface_record,
    face_radius,
    face_angle,
    face_axial,
    face_stagger,
    face_area,
    listeners,
    observer_group,
):
    passes = lax.axis_size("pass")
    cells = lax.axis_size("cell")
    pass_index = lax.axis_index("pass")
    cell_index = lax.axis_index("cell")
    passage_count = passes // 2
    half = pass_index % 2
    passage = pass_index // 2
    field = flow_state
    height = field.shape[0]
    width = field.shape[1]
    lower_levels = jnp.concatenate([field[None, 0, :], lagged_planes[0]], axis=0)
    upper_levels = jnp.concatenate([field[None, -1, :], lagged_planes[0]], axis=0)
    local_map = face_map[0] - cell_index * width
    after_lag = phase_lag[(passage + 1) % passage_count, 0]
    before_lag = phase_lag[(passage + passage_count - 1) % passage_count, 1]
    surfaces = []
    for level in range(STEPS):
        up_pick = jnp.where(half == 1, after_lag, 0)
        down_pick = jnp.where(half == 0, before_lag, 0)
        raw_low = shifted(upper_levels[up_pick], "pass", 1)
        raw_high = shifted(lower_levels[down_pick], "pass", -1)
        mapped = jnp.take(jnp.where(half == 0, raw_low, raw_high), local_map)
        ghost_low = jnp.where(half == 0, mapped, raw_low)
        ghost_high = jnp.where(half == 1, mapped, raw_high)
        field = relax(field, face_weights, forcing, ghost_low, ghost_high)
        lower_levels = jnp.concatenate([field[None, 0, :], lower_levels[:-1]], axis=0)
        upper_levels = jnp.concatenate([field[None, -1, :], upper_levels[:-1]], axis=0)
        surfaces.append(field[height // 2].astype(jnp.bfloat16))
    surface = jnp.concatenate([surface_record[0], jnp.stack(surfaces, axis=0)], axis=0)
    rate = time_rate(surface, 0)
    data = jnp.concatenate([surface, rate], axis=1)
    theta = passage.astype(jnp.float32) * (2.0 * math.pi / passage_count)
    scale = 64.0 / math.sqrt(width * cells * passes)
    radius = face_radius[half]
    angle = face_angle[half]
    axial = face_axial[half]
    stagger = face_stagger[half]
    area = face_area[half]
    per_cell = listeners.shape[1] // cells
    block = math.gcd(per_cell * lax.axis_size("cell"), 256)

    def one_block(offset):
        rows = offset * block + jnp.arange(block, dtype=jnp.int32)
        points = jnp.take(listeners, rows, axis=1)
        kernel = kernel_pair(points, theta, radius, angle, axial, stagger, area, scale)
        return lax.dot_general(
            kernel, data, (((1,), (1,)), ((), ())), preferred_element_type=jnp.float32
        )

    blocks = lax.map(
        one_block, jnp.arange(per_cell * lax.axis_size("cell") // block, dtype=jnp.int32)
    )
    share = lax.psum_scatter(
        blocks.reshape(per_cell * lax.axis_size("cell"), blocks.shape[-1]),
        "cell",
        scatter_dimension=0,
        tiled=True,
    )
    acoustic = lax.psum(share, "pass")
    labels = jnp.arange(GROUPS, dtype=jnp.int32)
    my_groups = lax.dynamic_slice_in_dim(observer_group, cell_index * per_cell, per_cell)
    member = (my_groups[None, :] == labels[:, None]).astype(jnp.float32)
    counts = jnp.sum((observer_group[None, :] == labels[:, None]).astype(jnp.float32), axis=1)
    partial_totals = jnp.dot(
        member, acoustic, precision=lax.Precision.HIGHEST, preferred_element_type=jnp.float32
    )
    totals = lax.psum(partial_totals, "cell")
    array_signal = totals / jnp.maximum(counts, 1.0)[:, None]
    return (field, acoustic, array_signal)


def solution(mesh):
    return jax.shard_map(
        on_device,
        mesh=mesh,
        in_specs=(
            P("pass", "cell"),
            P(None, "pass", "cell"),
            P("pass", "cell"),
            P("pass", None, "cell"),
            P(),
            P("pass", "cell"),
            P("pass", None, "cell"),
            P(None, "cell"),
            P(None, "cell"),
            P(None, "cell"),
            P(None, "cell"),
            P(None, "cell"),
            P(),
            P(),
        ),
        out_specs=(P("pass", "cell"), P("cell", None), P()),
        check_vma=False,
    )
```

profile of v0, /device:TPU:0, one launch (start us, length us, event | category | flops | bytes accessed | tf_op | source)
XLA Modules:
  0.0 348.3 jit_solution(7912482702422968674)
XLA Ops:
  8.5 2.4 collective-permute-start.2
  10.9 1.3 collective-permute-start.3
  12.2 1.3 constant_dynamic-slice_fusion.12
  16.5 2.4 collective-permute-start
  18.9 3.1 collective-permute-start.1
  22.1 3.2 fusion.109
  25.3 1.7 fusion.108
  28.6 4.5 %gather_fusion.1 = f32[1024]{0:T(1024)S(1)} fusion(f32[1024]{0:T(1024)S(1)} %broadcast_select_fusion.7, s32[1024]{0:T(1024)S(1)} %fusion.82), kind=kCustom, calls=%fused_computation.clone | custom fusion | bytes 12288 | tf_op jit(solution)/shard_map/jit(_take)/gather | solution.py:121
  33.2 5.1 %fusion.22 = (f32[256,1024]{1,0:T(8,128)S(1)}, f32[256,1024]{1,0:T(8,128)S(1)}) fusion(f32[256,1024]{1,0:T(8,128)S(1)} %copy-done, f32[255,1024]{1,0:T(8,128)} %get-tuple-element.332, f32[1,1024]{1,0:T(1,128)S(1)} %bitcast.169, f32[1,1024]{1,0:T(1,128)S(1)} %bitcast.172, f32[255,1024]{1,0:T(8,128)} %get-tuple-element.331, ...), kind=kLoop, calls=%fused_computation.51 | loop fusion | flops 4718592 | bytes 12582912 | tf_op jit(solution)/shard_map/add | solution.py:40
  38.5 1.5 fusion.106
  40.0 4.0 %collective-permute-start.6 = (f32[1,256]{1,0:T(1,128)S(1)}, f32[1,256]{1,0:T(1,128)S(1)}, u32[]{:S(2)}, u32[]{:S(2)}) collective-permute-start(f32[1,256]{1,0:T(1,128)S(1)} %bitcast.206), channel_id=1, source_target_pairs={{0,1},{1,2},{2,3},{4,5},{5,6},{6,7},{8,9},{9,10},{10,11},{12,13},{... | collective-permute-start | bytes 3080 | tf_op jit(solution)/shard_map/ppermute | solution.py:19
  44.0 1.3 collective-permute-start.7
  45.5 4.7 %collective-permute-start.5 = (f32[1024]{0:T(1024)S(1)}, f32[1024]{0:T(1024)S(1)}, u32[]{:S(2)}, u32[]{:S(2)}) collective-permute-start(f32[1024]{0:T(1024)S(1)} %bitcast.189), channel_id=1, source_target_pairs={{4,0},{8,4},{12,8},{16,12},{20,16},{24,20},{28,24},{0,28},{5,1},{9... | collective-permute-start | bytes 12296 | tf_op jit(solution)/shard_map/ppermute | solution.py:28
  50.2 1.7 fusion.105
  52.2 4.5 %gather_fusion.2 = f32[1024]{0:T(1024)S(1)} fusion(f32[1024]{0:T(1024)S(1)} %broadcast_select_fusion.6, s32[1024]{0:T(1024)S(1)} %fusion.82), kind=kCustom, calls=%fused_computation.2.clone | custom fusion | bytes 12288 | tf_op jit(solution)/shard_map/jit(_take)/gather | solution.py:121
  56.8 4.8 %fusion.27 = f32[256,1024]{1,0:T(8,128)S(1)} fusion(f32[256,1024]{1,0:T(8,128)S(1)} %copy-done, f32[255,1024]{1,0:T(8,128)} %get-tuple-element.326, f32[1,1024]{1,0:T(1,128)S(1)} %bitcast.174, f32[1,1024]{1,0:T(1,128)S(1)} %bitcast.173, f32[255,1024]{1,0:T(8,128)} %get-tuple-element.325, f32[256,1023]{1,0:T(8,128)} %get-tuple-element.324, ...), kind=kLoop, calls=%fused_computation.60 | loop fusion | flops 3670016 | bytes 12582912 | tf_op jit(solution)/shard_map/add | solution.py:40
  61.8 1.5 fusion.103
  63.3 4.1 %collective-permute-start.10 = (f32[1,256]{1,0:T(1,128)S(1)}, f32[1,256]{1,0:T(1,128)S(1)}, u32[]{:S(2)}, u32[]{:S(2)}) collective-permute-start(f32[1,256]{1,0:T(1,128)S(1)} %bitcast.216), channel_id=1, source_target_pairs={{0,1},{1,2},{2,3},{4,5},{5,6},{6,7},{8,9},{9,10},{10,11},{12,13},{... | collective-permute-start | bytes 3080 | tf_op jit(solution)/shard_map/ppermute | solution.py:19
  67.4 1.3 collective-permute-start.11
  68.8 4.8 %collective-permute-start.9 = (f32[1024]{0:T(1024)S(1)}, f32[1024]{0:T(1024)S(1)}, u32[]{:S(2)}, u32[]{:S(2)}) collective-permute-start(f32[1024]{0:T(1024)S(1)} %bitcast.198), channel_id=1, source_target_pairs={{4,0},{8,4},{12,8},{16,12},{20,16},{24,20},{28,24},{0,28},{5,1},{9... | collective-permute-start | bytes 12296 | tf_op jit(solution)/shard_map/ppermute | solution.py:28
  73.6 1.7 fusion.102
  75.6 4.5 %gather_fusion.3 = f32[1024]{0:T(1024)S(1)} fusion(f32[1024]{0:T(1024)S(1)} %broadcast_select_fusion.5, s32[1024]{0:T(1024)S(1)} %fusion.82), kind=kCustom, calls=%fused_computation.3.clone | custom fusion | bytes 12288 | tf_op jit(solution)/shard_map/jit(_take)/gather | solution.py:121
  80.1 5.1 %fusion.32 = f32[256,1024]{1,0:T(8,128)S(1)} fusion(f32[256,1024]{1,0:T(8,128)S(1)} %copy-done, f32[255,1024]{1,0:T(8,128)} %get-tuple-element.320, f32[1,1024]{1,0:T(1,128)S(1)} %bitcast.176, f32[1,1024]{1,0:T(1,128)S(1)} %bitcast.175, f32[255,1024]{1,0:T(8,128)} %get-tuple-element.319, f32[256,1023]{1,0:T(8,128)} %get-tuple-element.318, ...), kind=kLoop, calls=%fused_computation.69 | loop fusion | flops 3670016 | bytes 12582912 | tf_op jit(solution)/shard_map/add | solution.py:40
  85.4 1.5 fusion.100
  86.9 4.3 %collective-permute-start.14 = (f32[1,256]{1,0:T(1,128)S(1)}, f32[1,256]{1,0:T(1,128)S(1)}, u32[]{:S(2)}, u32[]{:S(2)}) collective-permute-start(f32[1,256]{1,0:T(1,128)S(1)} %bitcast.205), channel_id=1, source_target_pairs={{0,1},{1,2},{2,3},{4,5},{5,6},{6,7},{8,9},{9,10},{10,11},{12,13},{... | collective-permute-start | bytes 3080 | tf_op jit(solution)/shard_map/ppermute | solution.py:19
  92.6 4.7 %collective-permute-start.13 = (f32[1024]{0:T(1024)S(1)}, f32[1024]{0:T(1024)S(1)}, u32[]{:S(2)}, u32[]{:S(2)}) collective-permute-start(f32[1024]{0:T(1024)S(1)} %bitcast.190), channel_id=1, source_target_pairs={{4,0},{8,4},{12,8},{16,12},{20,16},{24,20},{28,24},{0,28},{5,1},{9... | collective-permute-start | bytes 12296 | tf_op jit(solution)/shard_map/ppermute | solution.py:28
  97.3 1.7 fusion.99
  99.4 4.5 %gather_fusion.4 = f32[1024]{0:T(1024)S(1)} fusion(f32[1024]{0:T(1024)S(1)} %broadcast_select_fusion.4, s32[1024]{0:T(1024)S(1)} %fusion.82), kind=kCustom, calls=%fused_computation.4.clone | custom fusion | bytes 12288 | tf_op jit(solution)/shard_map/jit(_take)/gather | solution.py:121
  103.9 4.8 %fusion.37 = f32[256,1024]{1,0:T(8,128)S(1)} fusion(f32[256,1024]{1,0:T(8,128)S(1)} %copy-done, f32[255,1024]{1,0:T(8,128)} %get-tuple-element.314, f32[1,1024]{1,0:T(1,128)S(1)} %bitcast.178, f32[1,1024]{1,0:T(1,128)S(1)} %bitcast.177, f32[255,1024]{1,0:T(8,128)} %get-tuple-element.313, f32[256,1023]{1,0:T(8,128)} %get-tuple-element.312, ...), kind=kLoop, calls=%fused_computation.78 | loop fusion | flops 3670016 | bytes 12582912 | tf_op jit(solution)/shard_map/add | solution.py:40
  108.9 1.5 fusion.97
  110.4 4.4 %collective-permute-start.18 = (f32[1,256]{1,0:T(1,128)S(1)}, f32[1,256]{1,0:T(1,128)S(1)}, u32[]{:S(2)}, u32[]{:S(2)}) collective-permute-start(f32[1,256]{1,0:T(1,128)S(1)} %bitcast.217), channel_id=1, source_target_pairs={{0,1},{1,2},{2,3},{4,5},{5,6},{6,7},{8,9},{9,10},{10,11},{12,13},{... | collective-permute-start | bytes 3080 | tf_op jit(solution)/shard_map/ppermute | solution.py:19
  114.8 1.3 collective-permute-start.19
  116.2 4.8 %collective-permute-start.17 = (f32[1024]{0:T(1024)S(1)}, f32[1024]{0:T(1024)S(1)}, u32[]{:S(2)}, u32[]{:S(2)}) collective-permute-start(f32[1024]{0:T(1024)S(1)} %bitcast.199), channel_id=1, source_target_pairs={{4,0},{8,4},{12,8},{16,12},{20,16},{24,20},{28,24},{0,28},{5,1},{9... | collective-permute-start | bytes 12296 | tf_op jit(solution)/shard_map/ppermute | solution.py:28
  121.0 1.7 fusion.96
  123.0 4.5 %gather_fusion.5 = f32[1024]{0:T(1024)S(1)} fusion(f32[1024]{0:T(1024)S(1)} %broadcast_select_fusion.3, s32[1024]{0:T(1024)S(1)} %fusion.82), kind=kCustom, calls=%fused_computation.5.clone | custom fusion | bytes 12288 | tf_op jit(solution)/shard_map/jit(_take)/gather | solution.py:121
  127.5 5.1 %fusion.42 = f32[256,1024]{1,0:T(8,128)S(1)} fusion(f32[256,1024]{1,0:T(8,128)S(1)} %copy-done, f32[255,1024]{1,0:T(8,128)} %get-tuple-element.308, f32[1,1024]{1,0:T(1,128)S(1)} %bitcast.180, f32[1,1024]{1,0:T(1,128)S(1)} %bitcast.179, f32[255,1024]{1,0:T(8,128)} %get-tuple-element.307, f32[256,1023]{1,0:T(8,128)} %get-tuple-element.306, ...), kind=kLoop, calls=%fused_computation.87 | loop fusion | flops 3670016 | bytes 12582912 | tf_op jit(solution)/shard_map/add | solution.py:40
  132.8 1.5 fusion.94
  134.3 4.2 %collective-permute-start.22 = (f32[1,256]{1,0:T(1,128)S(1)}, f32[1,256]{1,0:T(1,128)S(1)}, u32[]{:S(2)}, u32[]{:S(2)}) collective-permute-start(f32[1,256]{1,0:T(1,128)S(1)} %bitcast.207), channel_id=1, source_target_pairs={{0,1},{1,2},{2,3},{4,5},{5,6},{6,7},{8,9},{9,10},{10,11},{12,13},{... | collective-permute-start | bytes 3080 | tf_op jit(solution)/shard_map/ppermute | solution.py:19
  139.8 3.5 collective-permute-start.21
  143.4 1.7 fusion.93
  145.4 4.3 %collective-permute-done.20 = f32[1024]{0:T(1024)S(1)} collective-permute-done((f32[1024]{0:T(1024)S(1)}, f32[1024]{0:T(1024)S(1)}, u32[]{:S(2)}, u32[]{:S(2)}) %collective-permute-start.20) | collective-permute-done | bytes 4128 | tf_op jit(solution)/shard_map/ppermute | solution.py:28
  149.7 4.5 %gather_fusion.6 = f32[1024]{0:T(1024)S(1)} fusion(f32[1024]{0:T(1024)S(1)} %broadcast_select_fusion.2, s32[1024]{0:T(1024)S(1)} %fusion.82), kind=kCustom, calls=%fused_computation.6.clone | custom fusion | bytes 12288 | tf_op jit(solution)/shard_map/jit(_take)/gather | solution.py:121
  154.3 4.8 %fusion.47 = f32[256,1024]{1,0:T(8,128)S(1)} fusion(f32[256,1024]{1,0:T(8,128)S(1)} %copy-done, f32[255,1024]{1,0:T(8,128)} %get-tuple-element.302, f32[1,1024]{1,0:T(1,128)S(1)} %bitcast.182, f32[1,1024]{1,0:T(1,128)S(1)} %bitcast.181, f32[255,1024]{1,0:T(8,128)} %get-tuple-element.301, f32[256,1023]{1,0:T(8,128)} %get-tuple-element.300, ...), kind=kLoop, calls=%fused_computation.96 | loop fusion | flops 3670016 | bytes 12582912 | tf_op jit(solution)/shard_map/add | solution.py:40
  159.3 1.5 fusion.91
  160.8 4.3 %collective-permute-start.26 = (f32[1,256]{1,0:T(1,128)S(1)}, f32[1,256]{1,0:T(1,128)S(1)}, u32[]{:S(2)}, u32[]{:S(2)}) collective-permute-start(f32[1,256]{1,0:T(1,128)S(1)} %bitcast.218), channel_id=1, source_target_pairs={{0,1},{1,2},{2,3},{4,5},{5,6},{6,7},{8,9},{9,10},{10,11},{12,13},{... | collective-permute-start | bytes 3080 | tf_op jit(solution)/shard_map/ppermute | solution.py:19
  166.5 4.8 %collective-permute-start.25 = (f32[1024]{0:T(1024)S(1)}, f32[1024]{0:T(1024)S(1)}, u32[]{:S(2)}, u32[]{:S(2)}) collective-permute-start(f32[1024]{0:T(1024)S(1)} %bitcast.200), channel_id=1, source_target_pairs={{4,0},{8,4},{12,8},{16,12},{20,16},{24,20},{28,24},{0,28},{5,1},{9... | collective-permute-start | bytes 12296 | tf_op jit(solution)/shard_map/ppermute | solution.py:28
  171.2 1.7 fusion.90
  173.2 4.5 %gather_fusion.7 = f32[1024]{0:T(1024)S(1)} fusion(f32[1024]{0:T(1024)S(1)} %broadcast_select_fusion.1, s32[1024]{0:T(1024)S(1)} %fusion.82), kind=kCustom, calls=%fused_computation.7.clone | custom fusion | bytes 12288 | tf_op jit(solution)/shard_map/jit(_take)/gather | solution.py:121
  177.8 5.1 %fusion.52 = f32[256,1024]{1,0:T(8,128)S(1)} fusion(f32[256,1024]{1,0:T(8,128)S(1)} %copy-done, f32[255,1024]{1,0:T(8,128)} %get-tuple-element.296, f32[1,1024]{1,0:T(1,128)S(1)} %bitcast.184, f32[1,1024]{1,0:T(1,128)S(1)} %bitcast.183, f32[255,1024]{1,0:T(8,128)} %get-tuple-element.295, f32[256,1023]{1,0:T(8,128)} %get-tuple-element.294, ...), kind=kLoop, calls=%fused_computation.105 | loop fusion | flops 3670016 | bytes 12582912 | tf_op jit(solution)/shard_map/add | solution.py:40
  183.1 1.5 fusion.88
  184.6 5.1 %collective-permute-start.30 = (f32[1,256]{1,0:T(1,128)S(1)}, f32[1,256]{1,0:T(1,128)S(1)}, u32[]{:S(2)}, u32[]{:S(2)}) collective-permute-start(f32[1,256]{1,0:T(1,128)S(1)} %bitcast.210), channel_id=1, source_target_pairs={{0,1},{1,2},{2,3},{4,5},{5,6},{6,7},{8,9},{9,10},{10,11},{12,13},{... | collective-permute-start | bytes 3080 | tf_op jit(solution)/shard_map/ppermute | solution.py:19
  191.2 4.7 %collective-permute-start.29 = (f32[1024]{0:T(1024)S(1)}, f32[1024]{0:T(1024)S(1)}, u32[]{:S(2)}, u32[]{:S(2)}) collective-permute-start(f32[1024]{0:T(1024)S(1)} %bitcast.188), channel_id=1, source_target_pairs={{4,0},{8,4},{12,8},{16,12},{20,16},{24,20},{28,24},{0,28},{5,1},{9... | collective-permute-start | bytes 12296 | tf_op jit(solution)/shard_map/ppermute | solution.py:28
  195.9 1.7 fusion.87
  197.9 4.5 %gather_fusion.8 = f32[1024]{0:T(1024)S(1)} fusion(f32[1024]{0:T(1024)S(1)} %broadcast_select_fusion, s32[1024]{0:T(1024)S(1)} %fusion.82), kind=kCustom, calls=%fused_computation.8.clone | custom fusion | bytes 12288 | tf_op jit(solution)/shard_map/jit(_take)/gather | solution.py:121
  202.4 4.8 %fusion.57 = f32[256,1024]{1,0:T(8,128)S(1)} fusion(f32[256,1024]{1,0:T(8,128)S(1)} %copy-done, f32[255,1024]{1,0:T(8,128)} %get-tuple-element.290, f32[1,1024]{1,0:T(1,128)S(1)} %bitcast.171, f32[1,1024]{1,0:T(1,128)S(1)} %bitcast.170, f32[255,1024]{1,0:T(8,128)} %get-tuple-element.289, f32[256,1023]{1,0:T(8,128)} %get-tuple-element.288, ...), kind=kLoop, calls=%fused_computation.114 | loop fusion | flops 3670016 | bytes 12582912 | tf_op jit(solution)/shard_map/add | solution.py:40
  209.5 23.1 %while.13 = (s32[]{:T(128)}, f32[4,256,128]{2,1,0:T(8,128)}, f32[1024]{0:T(1024)S(1)}, f32[1,1024]{1,0:T(1,128)S(1)}, f32[]{:T(128)}, /*index=5*/f32[1024]{0:T(1...) while((s32[]{:T(128)}, f32[4,256,128]{2,1,0:T(8,128)}, ...), condition=%wide.region_1.3_spmd, body=%wide.region_0.2_spmd.sunk | while | flops 141568512 | bytes 2851517 | solution.py:149
  211.0 1.8 gather_fusion
  216.7 1.8 gather_fusion
  222.5 1.8 gather_fusion
  228.3 1.8 gather_fusion
  232.9 25.6 %reduce-scatter.2.cloned.1.call-done = f32[256,128]{1,0:T(8,128)} async-done(((f32[1024,128]{1,0:T(8,128)}), f32[256,128]{1,0:T(8,128)}) %reduce-scatter.2.cloned.1.call-update) | async-done | bytes 131088 | tf_op jit(solution)/shard_map/reduce_scatter | solution.py:152
  258.5 73.9 %all-reduce.2.cloned.1.call-done = f32[256,128]{1,0:T(8,128)} async-done(((f32[256,128]{1,0:T(8,128)}), f32[256,128]{1,0:T(8,128)}) %all-reduce.2.cloned.1.call-update) | async-done | bytes 131088 | tf_op jit(solution)/shard_map/psum | solution.py:158
  333.5 5.8 %psum.15 = f32[16,128]{1,0:T(8,128)S(1)} all-reduce(f32[16,128]{1,0:T(8,128)S(1)} %fusion.66), channel_id=1, replica_groups=mesh['pass'=8,'cell'=4] {'cell'}, use_global_device_ids=true, to_apply=%region_4.6 | all-reduce | flops 2048 | bytes 16384 | tf_op jit(solution)/shard_map/psum | solution.py:166
  339.9 1.6 copy.60
  (212 shorter events, 31.5 us)
Async XLA Ops:
  7.2 18.1 %copy-start.4 = (f32[256,1024]{1,0:T(8,128)S(1)}, f32[256,1024]{1,0:T(8,128)}, u32[]{:S(2)}) copy-start(f32[256,1024]{1,0:T(8,128)} %param.18) | copy-start | bytes 3145732
  7.2 251.3 %reduce-scatter.2.cloned.1.call-start = ((), (), s32[]{:S(2)}) async-start(), calls=%async_computation.1 | async-start | bytes 655360 | tf_op jit(solution)/shard_map/reduce_scatter | solution.py:152
  8.5 20.0 %collective-permute-start.2 = (f32[1,256]{1,0:T(1,128)S(1)}, f32[1,256]{1,0:T(1,128)S(1)}, u32[]{:S(2)}, u32[]{:S(2)}) collective-permute-start(f32[1,256]{1,0:T(1,128)S(1)} %bitcast.202), channel_id=1, source_target_pairs={{0,1},{1,2},{2,3},{4,5},{5,6},{6,7},{8,9},{9,10},{10,11},{12,13},{... | collective-permute-start | bytes 3080 | tf_op jit(solution)/shard_map/ppermute | solution.py:19
  10.9 17.4 %collective-permute-start.3 = (f32[1,256]{1,0:T(1,128)S(1)}, f32[1,256]{1,0:T(1,128)S(1)}, u32[]{:S(2)}, u32[]{:S(2)}) collective-permute-start(f32[1,256]{1,0:T(1,128)S(1)} %bitcast.203), channel_id=1, source_target_pairs={{1,0},{2,1},{3,2},{5,4},{6,5},{7,6},{9,8},{10,9},{11,10},{13,12},{... | collective-permute-start | bytes 3080 | tf_op jit(solution)/shard_map/ppermute | solution.py:20
  16.5 12.0 %collective-permute-start = (f32[1024]{0:T(1024)S(1)}, f32[1024]{0:T(1024)S(1)}, u32[]{:S(2)}, u32[]{:S(2)}) collective-permute-start(f32[1024]{0:T(1024)S(1)} %bitcast.186), channel_id=1, source_target_pairs={{28,0},{0,4},{4,8},{8,12},{12,16},{16,20},{20,24},{24,28},{29,1},{... | collective-permute-start | bytes 12296 | tf_op jit(solution)/shard_map/ppermute | solution.py:28
  18.9 9.7 %collective-permute-start.1 = (f32[1024]{0:T(1024)S(1)}, f32[1024]{0:T(1024)S(1)}, u32[]{:S(2)}, u32[]{:S(2)}) collective-permute-start(f32[1024]{0:T(1024)S(1)} %bitcast.185), channel_id=1, source_target_pairs={{4,0},{8,4},{12,8},{16,12},{20,16},{24,20},{28,24},{0,28},{5,1},{9... | collective-permute-start | bytes 12296 | tf_op jit(solution)/shard_map/ppermute | solution.py:28
  22.0 5.0 %copy-start.9 = (s32[1,1024]{1,0:T(1,128)S(1)}, s32[1,1024]{1,0:T(1,128)}, u32[]{:S(2)}) copy-start(s32[1,1024]{1,0:T(1,128)} %param.23) | copy-start | bytes 12292
  22.0 5.0 %copy-start.10 = (f32[2,1024]{1,0:T(2,128)S(1)}, f32[2,1024]{1,0:T(2,128)}, u32[]{:S(2)}) copy-start(f32[2,1024]{1,0:T(2,128)} %param.28) | copy-start | bytes 24580
  22.0 5.1 %copy-start.11 = (f32[2,1024]{1,0:T(2,128)S(1)}, f32[2,1024]{1,0:T(2,128)}, u32[]{:S(2)}) copy-start(f32[2,1024]{1,0:T(2,128)} %param.27) | copy-start | bytes 24580
  22.0 5.1 %copy-start.12 = (f32[2,1024]{1,0:T(2,128)S(1)}, f32[2,1024]{1,0:T(2,128)}, u32[]{:S(2)}) copy-start(f32[2,1024]{1,0:T(2,128)} %param.25) | copy-start | bytes 24580
  22.0 5.2 %copy-start.13 = (f32[2,1024]{1,0:T(2,128)S(1)}, f32[2,1024]{1,0:T(2,128)}, u32[]{:S(2)}) copy-start(f32[2,1024]{1,0:T(2,128)} %param.26) | copy-start | bytes 24580
  22.0 5.2 %copy-start.14 = (f32[2,1024]{1,0:T(2,128)S(1)}, f32[2,1024]{1,0:T(2,128)}, u32[]{:S(2)}) copy-start(f32[2,1024]{1,0:T(2,128)} %param.29) | copy-start | bytes 24580
  22.0 5.2 %copy-start.7 = (f32[3,1024]{1,0:T(4,128)S(1)}, f32[3,1024]{1,0:T(4,128)}, u32[]{:S(2)}) copy-start(f32[3,1024]{1,0:T(4,128)} %param.30) | copy-start | bytes 36868
  25.3 7.9 %copy-start = (f32[256,1024]{1,0:T(8,128)S(1)}, f32[256,1024]{1,0:T(8,128)}, u32[]{:S(2)}) copy-start(f32[256,1024]{1,0:T(8,128)} %param.20) | copy-start | bytes 3145732
  38.3 7.1 %copy-start.6 = (f32[1,8,1024]{2,1,0:T(8,128)S(1)}, f32[1,8,1024]{2,1,0:T(8,128)}, u32[]{:S(2)}) copy-start(f32[1,8,1024]{2,1,0:T(8,128)} %param.21) | copy-start | bytes 98308
  40.0 12.1 %collective-permute-start.6 = (f32[1,256]{1,0:T(1,128)S(1)}, f32[1,256]{1,0:T(1,128)S(1)}, u32[]{:S(2)}, u32[]{:S(2)}) collective-permute-start(f32[1,256]{1,0:T(1,128)S(1)} %bitcast.206), channel_id=1, source_target_pairs={{0,1},{1,2},{2,3},{4,5},{5,6},{6,7},{8,9},{9,10},{10,11},{12,13},{... | collective-permute-start | bytes 3080 | tf_op jit(solution)/shard_map/ppermute | solution.py:19
  44.0 7.9 %collective-permute-start.7 = (f32[1,256]{1,0:T(1,128)S(1)}, f32[1,256]{1,0:T(1,128)S(1)}, u32[]{:S(2)}, u32[]{:S(2)}) collective-permute-start(f32[1,256]{1,0:T(1,128)S(1)} %bitcast.211), channel_id=1, source_target_pairs={{1,0},{2,1},{3,2},{5,4},{6,5},{7,6},{9,8},{10,9},{11,10},{13,12},{... | collective-permute-start | bytes 3080 | tf_op jit(solution)/shard_map/ppermute | solution.py:20
  45.4 6.8 %collective-permute-start.4 = (f32[1024]{0:T(1024)S(1)}, f32[1024]{0:T(1024)S(1)}, u32[]{:S(2)}, u32[]{:S(2)}) collective-permute-start(f32[1024]{0:T(1024)S(1)} %bitcast.192), channel_id=1, source_target_pairs={{28,0},{0,4},{4,8},{8,12},{12,16},{16,20},{20,24},{24,28},{29,1},{... | collective-permute-start | bytes 12296 | tf_op jit(solution)/shard_map/ppermute | solution.py:28
  45.5 6.7 %collective-permute-start.5 = (f32[1024]{0:T(1024)S(1)}, f32[1024]{0:T(1024)S(1)}, u32[]{:S(2)}, u32[]{:S(2)}) collective-permute-start(f32[1024]{0:T(1024)S(1)} %bitcast.189), channel_id=1, source_target_pairs={{4,0},{8,4},{12,8},{16,12},{20,16},{24,20},{28,24},{0,28},{5,1},{9... | collective-permute-start | bytes 12296 | tf_op jit(solution)/shard_map/ppermute | solution.py:28
  61.6 13.7 %copy-start.1 = (f32[256,1024]{1,0:T(8,128)}, f32[256,1024]{1,0:T(8,128)S(1)}, u32[]{:S(2)}) copy-start(f32[256,1024]{1,0:T(8,128)S(1)} %fusion.27) | copy-start | bytes 3145732
  63.3 12.1 %collective-permute-start.10 = (f32[1,256]{1,0:T(1,128)S(1)}, f32[1,256]{1,0:T(1,128)S(1)}, u32[]{:S(2)}, u32[]{:S(2)}) collective-permute-start(f32[1,256]{1,0:T(1,128)S(1)} %bitcast.216), channel_id=1, source_target_pairs={{0,1},{1,2},{2,3},{4,5},{5,6},{6,7},{8,9},{9,10},{10,11},{12,13},{... | collective-permute-start | bytes 3080 | tf_op jit(solution)/shard_map/ppermute | solution.py:19
  67.4 7.9 %collective-permute-start.11 = (f32[1,256]{1,0:T(1,128)S(1)}, f32[1,256]{1,0:T(1,128)S(1)}, u32[]{:S(2)}, u32[]{:S(2)}) collective-permute-start(f32[1,256]{1,0:T(1,128)S(1)} %bitcast.222), channel_id=1, source_target_pairs={{1,0},{2,1},{3,2},{5,4},{6,5},{7,6},{9,8},{10,9},{11,10},{13,12},{... | collective-permute-start | bytes 3080 | tf_op jit(solution)/shard_map/ppermute | solution.py:20
  68.7 6.8 %collective-permute-start.8 = (f32[1024]{0:T(1024)S(1)}, f32[1024]{0:T(1024)S(1)}, u32[]{:S(2)}, u32[]{:S(2)}) collective-permute-start(f32[1024]{0:T(1024)S(1)} %bitcast.195), channel_id=1, source_target_pairs={{28,0},{0,4},{4,8},{8,12},{12,16},{16,20},{20,24},{24,28},{29,1},{... | collective-permute-start | bytes 12296 | tf_op jit(solution)/shard_map/ppermute | solution.py:28
  68.8 6.7 %collective-permute-start.9 = (f32[1024]{0:T(1024)S(1)}, f32[1024]{0:T(1024)S(1)}, u32[]{:S(2)}, u32[]{:S(2)}) collective-permute-start(f32[1024]{0:T(1024)S(1)} %bitcast.198), channel_id=1, source_target_pairs={{4,0},{8,4},{12,8},{16,12},{20,16},{24,20},{28,24},{0,28},{5,1},{9... | collective-permute-start | bytes 12296 | tf_op jit(solution)/shard_map/ppermute | solution.py:28
  86.9 12.3 %collective-permute-start.14 = (f32[1,256]{1,0:T(1,128)S(1)}, f32[1,256]{1,0:T(1,128)S(1)}, u32[]{:S(2)}, u32[]{:S(2)}) collective-permute-start(f32[1,256]{1,0:T(1,128)S(1)} %bitcast.205), channel_id=1, source_target_pairs={{0,1},{1,2},{2,3},{4,5},{5,6},{6,7},{8,9},{9,10},{10,11},{12,13},{... | collective-permute-start | bytes 3080 | tf_op jit(solution)/shard_map/ppermute | solution.py:19
  91.2 7.9 %collective-permute-start.15 = (f32[1,256]{1,0:T(1,128)S(1)}, f32[1,256]{1,0:T(1,128)S(1)}, u32[]{:S(2)}, u32[]{:S(2)}) collective-permute-start(f32[1,256]{1,0:T(1,128)S(1)} %bitcast.208), channel_id=1, source_target_pairs={{1,0},{2,1},{3,2},{5,4},{6,5},{7,6},{9,8},{10,9},{11,10},{13,12},{... | collective-permute-start | bytes 3080 | tf_op jit(solution)/shard_map/ppermute | solution.py:20
  92.6 6.8 %collective-permute-start.12 = (f32[1024]{0:T(1024)S(1)}, f32[1024]{0:T(1024)S(1)}, u32[]{:S(2)}, u32[]{:S(2)}) collective-permute-start(f32[1024]{0:T(1024)S(1)} %bitcast.193), channel_id=1, source_target_pairs={{28,0},{0,4},{4,8},{8,12},{12,16},{16,20},{20,24},{24,28},{29,1},{... | collective-permute-start | bytes 12296 | tf_op jit(solution)/shard_map/ppermute | solution.py:28
  92.6 6.7 %collective-permute-start.13 = (f32[1024]{0:T(1024)S(1)}, f32[1024]{0:T(1024)S(1)}, u32[]{:S(2)}, u32[]{:S(2)}) collective-permute-start(f32[1024]{0:T(1024)S(1)} %bitcast.190), channel_id=1, source_target_pairs={{4,0},{8,4},{12,8},{16,12},{20,16},{24,20},{28,24},{0,28},{5,1},{9... | collective-permute-start | bytes 12296 | tf_op jit(solution)/shard_map/ppermute | solution.py:28
  108.7 13.9 %copy-start.2 = (f32[256,1024]{1,0:T(8,128)}, f32[256,1024]{1,0:T(8,128)S(1)}, u32[]{:S(2)}) copy-start(f32[256,1024]{1,0:T(8,128)S(1)} %fusion.37) | copy-start | bytes 3145732
  110.4 12.4 %collective-permute-start.18 = (f32[1,256]{1,0:T(1,128)S(1)}, f32[1,256]{1,0:T(1,128)S(1)}, u32[]{:S(2)}, u32[]{:S(2)}) collective-permute-start(f32[1,256]{1,0:T(1,128)S(1)} %bitcast.217), channel_id=1, source_target_pairs={{0,1},{1,2},{2,3},{4,5},{5,6},{6,7},{8,9},{9,10},{10,11},{12,13},{... | collective-permute-start | bytes 3080 | tf_op jit(solution)/shard_map/ppermute | solution.py:19
  114.8 7.9 %collective-permute-start.19 = (f32[1,256]{1,0:T(1,128)S(1)}, f32[1,256]{1,0:T(1,128)S(1)}, u32[]{:S(2)}, u32[]{:S(2)}) collective-permute-start(f32[1,256]{1,0:T(1,128)S(1)} %bitcast.224), channel_id=1, source_target_pairs={{1,0},{2,1},{3,2},{5,4},{6,5},{7,6},{9,8},{10,9},{11,10},{13,12},{... | collective-permute-start | bytes 3080 | tf_op jit(solution)/shard_map/ppermute | solution.py:20
  116.1 6.8 %collective-permute-start.16 = (f32[1024]{0:T(1024)S(1)}, f32[1024]{0:T(1024)S(1)}, u32[]{:S(2)}, u32[]{:S(2)}) collective-permute-start(f32[1024]{0:T(1024)S(1)} %bitcast.196), channel_id=1, source_target_pairs={{28,0},{0,4},{4,8},{8,12},{12,16},{16,20},{20,24},{24,28},{29,1},{... | collective-permute-start | bytes 12296 | tf_op jit(solution)/shard_map/ppermute | solution.py:28
  116.2 6.7 %collective-permute-start.17 = (f32[1024]{0:T(1024)S(1)}, f32[1024]{0:T(1024)S(1)}, u32[]{:S(2)}, u32[]{:S(2)}) collective-permute-start(f32[1024]{0:T(1024)S(1)} %bitcast.199), channel_id=1, source_target_pairs={{4,0},{8,4},{12,8},{16,12},{20,16},{24,20},{28,24},{0,28},{5,1},{9... | collective-permute-start | bytes 12296 | tf_op jit(solution)/shard_map/ppermute | solution.py:28
  134.3 11.0 %collective-permute-start.22 = (f32[1,256]{1,0:T(1,128)S(1)}, f32[1,256]{1,0:T(1,128)S(1)}, u32[]{:S(2)}, u32[]{:S(2)}) collective-permute-start(f32[1,256]{1,0:T(1,128)S(1)} %bitcast.207), channel_id=1, source_target_pairs={{0,1},{1,2},{2,3},{4,5},{5,6},{6,7},{8,9},{9,10},{10,11},{12,13},{... | collective-permute-start | bytes 3080 | tf_op jit(solution)/shard_map/ppermute | solution.py:19
  138.5 6.6 %collective-permute-start.23 = (f32[1,256]{1,0:T(1,128)S(1)}, f32[1,256]{1,0:T(1,128)S(1)}, u32[]{:S(2)}, u32[]{:S(2)}) collective-permute-start(f32[1,256]{1,0:T(1,128)S(1)} %bitcast.213), channel_id=1, source_target_pairs={{1,0},{2,1},{3,2},{5,4},{6,5},{7,6},{9,8},{10,9},{11,10},{13,12},{... | collective-permute-start | bytes 3080 | tf_op jit(solution)/shard_map/ppermute | solution.py:20
  139.8 5.6 %collective-permute-start.21 = (f32[1024]{0:T(1024)S(1)}, f32[1024]{0:T(1024)S(1)}, u32[]{:S(2)}, u32[]{:S(2)}) collective-permute-start(f32[1024]{0:T(1024)S(1)} %bitcast.191), channel_id=1, source_target_pairs={{4,0},{8,4},{12,8},{16,12},{20,16},{24,20},{28,24},{0,28},{5,1},{9... | collective-permute-start | bytes 12296 | tf_op jit(solution)/shard_map/ppermute | solution.py:28
  143.4 6.4 %collective-permute-start.20 = (f32[1024]{0:T(1024)S(1)}, f32[1024]{0:T(1024)S(1)}, u32[]{:S(2)}, u32[]{:S(2)}) collective-permute-start(f32[1024]{0:T(1024)S(1)} %bitcast.194), channel_id=1, source_target_pairs={{28,0},{0,4},{4,8},{8,12},{12,16},{16,20},{20,24},{24,28},{29,1},{... | collective-permute-start | bytes 12296 | tf_op jit(solution)/shard_map/ppermute | solution.py:28
  159.1 13.8 %copy-start.3 = (f32[256,1024]{1,0:T(8,128)}, f32[256,1024]{1,0:T(8,128)S(1)}, u32[]{:S(2)}) copy-start(f32[256,1024]{1,0:T(8,128)S(1)} %fusion.47) | copy-start | bytes 3145732
  160.8 12.3 %collective-permute-start.26 = (f32[1,256]{1,0:T(1,128)S(1)}, f32[1,256]{1,0:T(1,128)S(1)}, u32[]{:S(2)}, u32[]{:S(2)}) collective-permute-start(f32[1,256]{1,0:T(1,128)S(1)} %bitcast.218), channel_id=1, source_target_pairs={{0,1},{1,2},{2,3},{4,5},{5,6},{6,7},{8,9},{9,10},{10,11},{12,13},{... | collective-permute-start | bytes 3080 | tf_op jit(solution)/shard_map/ppermute | solution.py:19
  165.0 7.9 %collective-permute-start.27 = (f32[1,256]{1,0:T(1,128)S(1)}, f32[1,256]{1,0:T(1,128)S(1)}, u32[]{:S(2)}, u32[]{:S(2)}) collective-permute-start(f32[1,256]{1,0:T(1,128)S(1)} %bitcast.226), channel_id=1, source_target_pairs={{1,0},{2,1},{3,2},{5,4},{6,5},{7,6},{9,8},{10,9},{11,10},{13,12},{... | collective-permute-start | bytes 3080 | tf_op jit(solution)/shard_map/ppermute | solution.py:20
  166.4 6.8 %collective-permute-start.24 = (f32[1024]{0:T(1024)S(1)}, f32[1024]{0:T(1024)S(1)}, u32[]{:S(2)}, u32[]{:S(2)}) collective-permute-start(f32[1024]{0:T(1024)S(1)} %bitcast.197), channel_id=1, source_target_pairs={{28,0},{0,4},{4,8},{8,12},{12,16},{16,20},{20,24},{24,28},{29,1},{... | collective-permute-start | bytes 12296 | tf_op jit(solution)/shard_map/ppermute | solution.py:28
  166.5 6.7 %collective-permute-start.25 = (f32[1024]{0:T(1024)S(1)}, f32[1024]{0:T(1024)S(1)}, u32[]{:S(2)}, u32[]{:S(2)}) collective-permute-start(f32[1024]{0:T(1024)S(1)} %bitcast.200), channel_id=1, source_target_pairs={{4,0},{8,4},{12,8},{16,12},{20,16},{24,20},{28,24},{0,28},{5,1},{9... | collective-permute-start | bytes 12296 | tf_op jit(solution)/shard_map/ppermute | solution.py:28
  184.6 13.0 %collective-permute-start.30 = (f32[1,256]{1,0:T(1,128)S(1)}, f32[1,256]{1,0:T(1,128)S(1)}, u32[]{:S(2)}, u32[]{:S(2)}) collective-permute-start(f32[1,256]{1,0:T(1,128)S(1)} %bitcast.210), channel_id=1, source_target_pairs={{0,1},{1,2},{2,3},{4,5},{5,6},{6,7},{8,9},{9,10},{10,11},{12,13},{... | collective-permute-start | bytes 3080 | tf_op jit(solution)/shard_map/ppermute | solution.py:19
  189.8 7.7 %collective-permute-start.31 = (f32[1,256]{1,0:T(1,128)S(1)}, f32[1,256]{1,0:T(1,128)S(1)}, u32[]{:S(2)}, u32[]{:S(2)}) collective-permute-start(f32[1,256]{1,0:T(1,128)S(1)} %bitcast.215), channel_id=1, source_target_pairs={{1,0},{2,1},{3,2},{5,4},{6,5},{7,6},{9,8},{10,9},{11,10},{13,12},{... | collective-permute-start | bytes 3080 | tf_op jit(solution)/shard_map/ppermute | solution.py:20
  191.1 6.7 %collective-permute-start.28 = (f32[1024]{0:T(1024)S(1)}, f32[1024]{0:T(1024)S(1)}, u32[]{:S(2)}, u32[]{:S(2)}) collective-permute-start(f32[1024]{0:T(1024)S(1)} %bitcast.187), channel_id=1, source_target_pairs={{28,0},{0,4},{4,8},{8,12},{12,16},{16,20},{20,24},{24,28},{29,1},{... | collective-permute-start | bytes 12296 | tf_op jit(solution)/shard_map/ppermute | solution.py:28
  191.2 6.7 %collective-permute-start.29 = (f32[1024]{0:T(1024)S(1)}, f32[1024]{0:T(1024)S(1)}, u32[]{:S(2)}, u32[]{:S(2)}) collective-permute-start(f32[1024]{0:T(1024)S(1)} %bitcast.188), channel_id=1, source_target_pairs={{4,0},{8,4},{12,8},{16,12},{20,16},{24,20},{28,24},{0,28},{5,1},{9... | collective-permute-start | bytes 12296 | tf_op jit(solution)/shard_map/ppermute | solution.py:28
  207.2 1.0 copy-start.5
  209.5 23.2 %copy-start.8 = (s32[1024]{0:T(1024)S(1)}, s32[1024]{0:T(1024)}, u32[]{:S(2)}) copy-start(s32[1024]{0:T(1024)} %param.31) | copy-start | bytes 12292
  232.7 99.7 %all-reduce.2.cloned.1.call-start = ((), (), s32[]{:S(2)}) async-start(), calls=%async_computation.2 | async-start | bytes 262144 | tf_op jit(solution)/shard_map/psum | solution.py:158
Sparse Core Ops, SparseCore 0:
  232.8 25.6 reduce-scatter.1
  261.8 70.4 all-reduce.1
where the time goes:
time: 349 us; the launch traced here: 348 us
  waiting for transfers between devices  104 us (30%)
  local copies, waits for them, and re-layouts  85.8 us (25%)
  starting transfers between devices  80.9 us (23%)
  other arithmetic  47.1 us (13%)
  between operations  16.7 us (5%)
  blocking collectives  5.77 us (2%)
  matrix products  5.43 us (2%)
    psum x1, waiting for transfers between devices, on_device(): acoustic = lax.psum(share, 'pass')  73.9 us
    add x8, other arithmetic, relax(): keep * field + coeff[0] * below + coeff[1] * above + coeff[2] * left  39.5 us
    ppermute x16, starting transfers between devices, shifted(): return lax.ppermute(block, axis, route)  37.7 us
    gather x8, local copies, waits for them, and re-layouts, on_device(): mapped = jnp.take(jnp.where(half == 0, raw_low, raw_high), local_map)  36.2 us
    ppermute x8, starting transfers between devices, padded(): before = lax.ppermute(last, axis, up)  32.7 us
    reduce_scatter x1, waiting for transfers between devices, on_device(): lax.psum_scatter(blocks.reshape(per_cell * lax.axis_size('cell'), blocks....  25.6 us
    slice x8, local copies, waits for them, and re-layouts, relax(): above = jnp.concatenate([field[1:, :], ghost_high[None, :]], axis=0)  13.6 us
    slice x8, local copies, waits for them, and re-layouts, relax(): right = jnp.concatenate([field[:, 1:], rim[3][:, None]], axis=1)  13.3 us
  transfers between devices with their start and end apart: 34, of which 3 were waited for; matrix products, arithmetic and copies ran while one was open for 7% of the time, Pallas kernels for 0%

commit v1 on v0

--- a/solution.py
+++ b/solution.py
@@ -155,7 +155,7 @@
         scatter_dimension=0,
         tiled=True,
     )
-    acoustic = lax.psum(share, "pass")
+    acoustic = jnp.sum(lax.all_gather(share, "pass"), axis=0)
     labels = jnp.arange(GROUPS, dtype=jnp.int32)
     my_groups = lax.dynamic_slice_in_dim(observer_group, cell_index * per_cell, per_cell)
     member = (my_groups[None, :] == labels[:, None]).astype(jnp.float32)

time: 349 us -> 316 us (0.905)
  waiting for transfers between devices: 104 us -> 72.4 us
    psum x1 -> x0, waiting for transfers between devices: 73.9 us -> none  [on_device(): acoustic = lax.psum(share, 'pass')]
    all_gather x0 -> x1, waiting for transfers between devices: none -> 42.2 us  [on_device(): acoustic = jnp.sum(lax.all_gather(share, 'pass'), axis=0)]
where the time goes in v1:
time: 316 us; the launch traced here: 315 us
  local copies, waits for them, and re-layouts  84 us (27%)
  starting transfers between devices  80.9 us (26%)
  waiting for transfers between devices  72.4 us (23%)
  other arithmetic  48.3 us (15%)
  between operations  16.7 us (5%)
  blocking collectives  5.77 us (2%)
  matrix products  4.59 us (1%)
    all_gather x1, waiting for transfers between devices, on_device(): acoustic = jnp.sum(lax.all_gather(share, 'pass'), axis=0)  42.2 us
    add x8, other arithmetic, relax(): keep * field + coeff[0] * below + coeff[1] * above + coeff[2] * left  39.4 us
    ppermute x16, starting transfers between devices, shifted(): return lax.ppermute(block, axis, route)  37.7 us
    gather x8, local copies, waits for them, and re-layouts, on_device(): mapped = jnp.take(jnp.where(half == 0, raw_low, raw_high), local_map)  36.2 us
    ppermute x8, starting transfers between devices, padded(): before = lax.ppermute(last, axis, up)  32.7 us
    reduce_scatter x1, waiting for transfers between devices, on_device(): lax.psum_scatter(blocks.reshape(per_cell * lax.axis_size('cell'), blocks....  25.8 us
    slice x8, local copies, waits for them, and re-layouts, relax(): above = jnp.concatenate([field[1:, :], ghost_high[None, :]], axis=0)  13.6 us
    slice x8, local copies, waits for them, and re-layouts, relax(): right = jnp.concatenate([field[:, 1:], rim[3][:, None]], axis=1)  13.3 us
  transfers between devices with their start and end apart: 34, of which 3 were waited for; matrix products, arithmetic and copies ran while one was open for 7% of the time, Pallas kernels for 0%

profile of v1, /device:TPU:0, one launch (start us, length us, event | category | flops | bytes accessed | tf_op | source)
XLA Modules:
  0.0 315.0 jit_solution(4284122152658025209)
XLA Ops:
  8.5 2.4 collective-permute-start.2
  10.9 1.3 collective-permute-start.3
  12.2 1.3 constant_dynamic-slice_fusion.12
  16.5 2.4 collective-permute-start
  18.9 3.1 collective-permute-start.1
  22.1 3.2 %fusion.109 = (f32[255,1024]{1,0:T(8,128)}, f32[255,1024]{1,0:T(8,128)}) fusion(f32[256,1024]{1,0:T(8,128)} %param.18), kind=kLoop, calls=%fused_computation.273 | loop fusion | bytes 4177920 | tf_op jit(solution)/shard_map/slice | solution.py:35
  25.3 1.7 fusion.108
  28.6 4.5 %gather_fusion.1 = f32[1024]{0:T(1024)S(1)} fusion(f32[1024]{0:T(1024)S(1)} %broadcast_select_fusion.7, s32[1024]{0:T(1024)S(1)} %fusion.82), kind=kCustom, calls=%fused_computation.clone | custom fusion | bytes 12288 | tf_op jit(solution)/shard_map/jit(_take)/gather | solution.py:121
  33.2 5.0 %fusion.22 = (f32[256,1024]{1,0:T(8,128)S(1)}, f32[256,1024]{1,0:T(8,128)S(1)}) fusion(f32[256,1024]{1,0:T(8,128)S(1)} %copy-done, f32[255,1024]{1,0:T(8,128)} %get-tuple-element.332, f32[1,1024]{1,0:T(1,128)S(1)} %bitcast.171, f32[1,1024]{1,0:T(1,128)S(1)} %bitcast.174, f32[255,1024]{1,0:T(8,128)} %get-tuple-element.331, ...), kind=kLoop, calls=%fused_computation.51 | loop fusion | flops 4718592 | bytes 12582912 | tf_op jit(solution)/shard_map/add | solution.py:40
  38.4 1.5 fusion.106
  39.9 4.0 %collective-permute-start.6 = (f32[1,256]{1,0:T(1,128)S(1)}, f32[1,256]{1,0:T(1,128)S(1)}, u32[]{:S(2)}, u32[]{:S(2)}) collective-permute-start(f32[1,256]{1,0:T(1,128)S(1)} %bitcast.208), channel_id=1, source_target_pairs={{0,1},{1,2},{2,3},{4,5},{5,6},{6,7},{8,9},{9,10},{10,11},{12,13},{... | collective-permute-start | bytes 3080 | tf_op jit(solution)/shard_map/ppermute | solution.py:19
  43.9 1.3 collective-permute-start.7
  45.4 4.7 %collective-permute-start.5 = (f32[1024]{0:T(1024)S(1)}, f32[1024]{0:T(1024)S(1)}, u32[]{:S(2)}, u32[]{:S(2)}) collective-permute-start(f32[1024]{0:T(1024)S(1)} %bitcast.191), channel_id=1, source_target_pairs={{4,0},{8,4},{12,8},{16,12},{20,16},{24,20},{28,24},{0,28},{5,1},{9... | collective-permute-start | bytes 12296 | tf_op jit(solution)/shard_map/ppermute | solution.py:28
  50.1 1.7 fusion.105
  52.1 4.5 %gather_fusion.2 = f32[1024]{0:T(1024)S(1)} fusion(f32[1024]{0:T(1024)S(1)} %broadcast_select_fusion.6, s32[1024]{0:T(1024)S(1)} %fusion.82), kind=kCustom, calls=%fused_computation.2.clone | custom fusion | bytes 12288 | tf_op jit(solution)/shard_map/jit(_take)/gather | solution.py:121
  56.7 4.8 %fusion.27 = f32[256,1024]{1,0:T(8,128)S(1)} fusion(f32[256,1024]{1,0:T(8,128)S(1)} %copy-done, f32[255,1024]{1,0:T(8,128)} %get-tuple-element.326, f32[1,1024]{1,0:T(1,128)S(1)} %bitcast.176, f32[1,1024]{1,0:T(1,128)S(1)} %bitcast.175, f32[255,1024]{1,0:T(8,128)} %get-tuple-element.325, f32[256,1023]{1,0:T(8,128)} %get-tuple-element.324, ...), kind=kLoop, calls=%fused_computation.60 | loop fusion | flops 3670016 | bytes 12582912 | tf_op jit(solution)/shard_map/add | solution.py:40
  61.7 1.5 fusion.103
  63.2 4.1 %collective-permute-start.10 = (f32[1,256]{1,0:T(1,128)S(1)}, f32[1,256]{1,0:T(1,128)S(1)}, u32[]{:S(2)}, u32[]{:S(2)}) collective-permute-start(f32[1,256]{1,0:T(1,128)S(1)} %bitcast.218), channel_id=1, source_target_pairs={{0,1},{1,2},{2,3},{4,5},{5,6},{6,7},{8,9},{9,10},{10,11},{12,13},{... | collective-permute-start | bytes 3080 | tf_op jit(solution)/shard_map/ppermute | solution.py:19
  67.3 1.3 collective-permute-start.11
  68.7 4.8 %collective-permute-start.9 = (f32[1024]{0:T(1024)S(1)}, f32[1024]{0:T(1024)S(1)}, u32[]{:S(2)}, u32[]{:S(2)}) collective-permute-start(f32[1024]{0:T(1024)S(1)} %bitcast.200), channel_id=1, source_target_pairs={{4,0},{8,4},{12,8},{16,12},{20,16},{24,20},{28,24},{0,28},{5,1},{9... | collective-permute-start | bytes 12296 | tf_op jit(solution)/shard_map/ppermute | solution.py:28
  73.5 1.7 fusion.102
  75.5 4.5 %gather_fusion.3 = f32[1024]{0:T(1024)S(1)} fusion(f32[1024]{0:T(1024)S(1)} %broadcast_select_fusion.5, s32[1024]{0:T(1024)S(1)} %fusion.82), kind=kCustom, calls=%fused_computation.3.clone | custom fusion | bytes 12288 | tf_op jit(solution)/shard_map/jit(_take)/gather | solution.py:121
  80.1 5.1 %fusion.32 = f32[256,1024]{1,0:T(8,128)S(1)} fusion(f32[256,1024]{1,0:T(8,128)S(1)} %copy-done, f32[255,1024]{1,0:T(8,128)} %get-tuple-element.320, f32[1,1024]{1,0:T(1,128)S(1)} %bitcast.178, f32[1,1024]{1,0:T(1,128)S(1)} %bitcast.177, f32[255,1024]{1,0:T(8,128)} %get-tuple-element.319, f32[256,1023]{1,0:T(8,128)} %get-tuple-element.318, ...), kind=kLoop, calls=%fused_computation.69 | loop fusion | flops 3670016 | bytes 12582912 | tf_op jit(solution)/shard_map/add | solution.py:40
  85.4 1.5 fusion.100
  86.8 4.3 %collective-permute-start.14 = (f32[1,256]{1,0:T(1,128)S(1)}, f32[1,256]{1,0:T(1,128)S(1)}, u32[]{:S(2)}, u32[]{:S(2)}) collective-permute-start(f32[1,256]{1,0:T(1,128)S(1)} %bitcast.207), channel_id=1, source_target_pairs={{0,1},{1,2},{2,3},{4,5},{5,6},{6,7},{8,9},{9,10},{10,11},{12,13},{... | collective-permute-start | bytes 3080 | tf_op jit(solution)/shard_map/ppermute | solution.py:19
  91.1 1.3 collective-permute-start.15
  92.6 4.7 %collective-permute-start.13 = (f32[1024]{0:T(1024)S(1)}, f32[1024]{0:T(1024)S(1)}, u32[]{:S(2)}, u32[]{:S(2)}) collective-permute-start(f32[1024]{0:T(1024)S(1)} %bitcast.192), channel_id=1, source_target_pairs={{4,0},{8,4},{12,8},{16,12},{20,16},{24,20},{28,24},{0,28},{5,1},{9... | collective-permute-start | bytes 12296 | tf_op jit(solution)/shard_map/ppermute | solution.py:28
  97.3 1.7 fusion.99
  99.3 4.5 %gather_fusion.4 = f32[1024]{0:T(1024)S(1)} fusion(f32[1024]{0:T(1024)S(1)} %broadcast_select_fusion.4, s32[1024]{0:T(1024)S(1)} %fusion.82), kind=kCustom, calls=%fused_computation.4.clone | custom fusion | bytes 12288 | tf_op jit(solution)/shard_map/jit(_take)/gather | solution.py:121
  103.8 4.8 %fusion.37 = f32[256,1024]{1,0:T(8,128)S(1)} fusion(f32[256,1024]{1,0:T(8,128)S(1)} %copy-done, f32[255,1024]{1,0:T(8,128)} %get-tuple-element.314, f32[1,1024]{1,0:T(1,128)S(1)} %bitcast.180, f32[1,1024]{1,0:T(1,128)S(1)} %bitcast.179, f32[255,1024]{1,0:T(8,128)} %get-tuple-element.313, f32[256,1023]{1,0:T(8,128)} %get-tuple-element.312, ...), kind=kLoop, calls=%fused_computation.78 | loop fusion | flops 3670016 | bytes 12582912 | tf_op jit(solution)/shard_map/add | solution.py:40
  108.9 1.5 fusion.97
  110.4 4.3 %collective-permute-start.18 = (f32[1,256]{1,0:T(1,128)S(1)}, f32[1,256]{1,0:T(1,128)S(1)}, u32[]{:S(2)}, u32[]{:S(2)}) collective-permute-start(f32[1,256]{1,0:T(1,128)S(1)} %bitcast.219), channel_id=1, source_target_pairs={{0,1},{1,2},{2,3},{4,5},{5,6},{6,7},{8,9},{9,10},{10,11},{12,13},{... | collective-permute-start | bytes 3080 | tf_op jit(solution)/shard_map/ppermute | solution.py:19
  114.7 1.3 collective-permute-start.19
  116.2 4.8 %collective-permute-start.17 = (f32[1024]{0:T(1024)S(1)}, f32[1024]{0:T(1024)S(1)}, u32[]{:S(2)}, u32[]{:S(2)}) collective-permute-start(f32[1024]{0:T(1024)S(1)} %bitcast.201), channel_id=1, source_target_pairs={{4,0},{8,4},{12,8},{16,12},{20,16},{24,20},{28,24},{0,28},{5,1},{9... | collective-permute-start | bytes 12296 | tf_op jit(solution)/shard_map/ppermute | solution.py:28
  120.9 1.7 fusion.96
  122.9 4.5 %gather_fusion.5 = f32[1024]{0:T(1024)S(1)} fusion(f32[1024]{0:T(1024)S(1)} %broadcast_select_fusion.3, s32[1024]{0:T(1024)S(1)} %fusion.82), kind=kCustom, calls=%fused_computation.5.clone | custom fusion | bytes 12288 | tf_op jit(solution)/shard_map/jit(_take)/gather | solution.py:121
  127.5 5.1 %fusion.42 = f32[256,1024]{1,0:T(8,128)S(1)} fusion(f32[256,1024]{1,0:T(8,128)S(1)} %copy-done, f32[255,1024]{1,0:T(8,128)} %get-tuple-element.308, f32[1,1024]{1,0:T(1,128)S(1)} %bitcast.182, f32[1,1024]{1,0:T(1,128)S(1)} %bitcast.181, f32[255,1024]{1,0:T(8,128)} %get-tuple-element.307, f32[256,1023]{1,0:T(8,128)} %get-tuple-element.306, ...), kind=kLoop, calls=%fused_computation.87 | loop fusion | flops 3670016 | bytes 12582912 | tf_op jit(solution)/shard_map/add | solution.py:40
  132.8 1.5 fusion.94
  134.3 4.2 %collective-permute-start.22 = (f32[1,256]{1,0:T(1,128)S(1)}, f32[1,256]{1,0:T(1,128)S(1)}, u32[]{:S(2)}, u32[]{:S(2)}) collective-permute-start(f32[1,256]{1,0:T(1,128)S(1)} %bitcast.209), channel_id=1, source_target_pairs={{0,1},{1,2},{2,3},{4,5},{5,6},{6,7},{8,9},{9,10},{10,11},{12,13},{... | collective-permute-start | bytes 3080 | tf_op jit(solution)/shard_map/ppermute | solution.py:19
  139.8 3.5 %collective-permute-start.21 = (f32[1024]{0:T(1024)S(1)}, f32[1024]{0:T(1024)S(1)}, u32[]{:S(2)}, u32[]{:S(2)}) collective-permute-start(f32[1024]{0:T(1024)S(1)} %bitcast.193), channel_id=1, source_target_pairs={{4,0},{8,4},{12,8},{16,12},{20,16},{24,20},{28,24},{0,28},{5,1},{9... | collective-permute-start | bytes 12296 | tf_op jit(solution)/shard_map/ppermute | solution.py:28
  143.4 1.7 fusion.93
  145.4 4.3 %collective-permute-done.20 = f32[1024]{0:T(1024)S(1)} collective-permute-done((f32[1024]{0:T(1024)S(1)}, f32[1024]{0:T(1024)S(1)}, u32[]{:S(2)}, u32[]{:S(2)}) %collective-permute-start.20) | collective-permute-done | bytes 4128 | tf_op jit(solution)/shard_map/ppermute | solution.py:28
  149.7 4.5 %gather_fusion.6 = f32[1024]{0:T(1024)S(1)} fusion(f32[1024]{0:T(1024)S(1)} %broadcast_select_fusion.2, s32[1024]{0:T(1024)S(1)} %fusion.82), kind=kCustom, calls=%fused_computation.6.clone | custom fusion | bytes 12288 | tf_op jit(solution)/shard_map/jit(_take)/gather | solution.py:121
  154.2 4.8 %fusion.47 = f32[256,1024]{1,0:T(8,128)S(1)} fusion(f32[256,1024]{1,0:T(8,128)S(1)} %copy-done, f32[255,1024]{1,0:T(8,128)} %get-tuple-element.302, f32[1,1024]{1,0:T(1,128)S(1)} %bitcast.184, f32[1,1024]{1,0:T(1,128)S(1)} %bitcast.183, f32[255,1024]{1,0:T(8,128)} %get-tuple-element.301, f32[256,1023]{1,0:T(8,128)} %get-tuple-element.300, ...), kind=kLoop, calls=%fused_computation.96 | loop fusion | flops 3670016 | bytes 12582912 | tf_op jit(solution)/shard_map/add | solution.py:40
  159.2 1.5 fusion.91
  160.7 4.3 %collective-permute-start.26 = (f32[1,256]{1,0:T(1,128)S(1)}, f32[1,256]{1,0:T(1,128)S(1)}, u32[]{:S(2)}, u32[]{:S(2)}) collective-permute-start(f32[1,256]{1,0:T(1,128)S(1)} %bitcast.220), channel_id=1, source_target_pairs={{0,1},{1,2},{2,3},{4,5},{5,6},{6,7},{8,9},{9,10},{10,11},{12,13},{... | collective-permute-start | bytes 3080 | tf_op jit(solution)/shard_map/ppermute | solution.py:19
  166.4 4.8 %collective-permute-start.25 = (f32[1024]{0:T(1024)S(1)}, f32[1024]{0:T(1024)S(1)}, u32[]{:S(2)}, u32[]{:S(2)}) collective-permute-start(f32[1024]{0:T(1024)S(1)} %bitcast.202), channel_id=1, source_target_pairs={{4,0},{8,4},{12,8},{16,12},{20,16},{24,20},{28,24},{0,28},{5,1},{9... | collective-permute-start | bytes 12296 | tf_op jit(solution)/shard_map/ppermute | solution.py:28
  171.2 1.7 fusion.90
  173.2 4.5 %gather_fusion.7 = f32[1024]{0:T(1024)S(1)} fusion(f32[1024]{0:T(1024)S(1)} %broadcast_select_fusion.1, s32[1024]{0:T(1024)S(1)} %fusion.82), kind=kCustom, calls=%fused_computation.7.clone | custom fusion | bytes 12288 | tf_op jit(solution)/shard_map/jit(_take)/gather | solution.py:121
  177.7 5.1 %fusion.52 = f32[256,1024]{1,0:T(8,128)S(1)} fusion(f32[256,1024]{1,0:T(8,128)S(1)} %copy-done, f32[255,1024]{1,0:T(8,128)} %get-tuple-element.296, f32[1,1024]{1,0:T(1,128)S(1)} %bitcast.186, f32[1,1024]{1,0:T(1,128)S(1)} %bitcast.185, f32[255,1024]{1,0:T(8,128)} %get-tuple-element.295, f32[256,1023]{1,0:T(8,128)} %get-tuple-element.294, ...), kind=kLoop, calls=%fused_computation.105 | loop fusion | flops 3670016 | bytes 12582912 | tf_op jit(solution)/shard_map/add | solution.py:40
  183.0 1.5 fusion.88
  184.6 5.1 %collective-permute-start.30 = (f32[1,256]{1,0:T(1,128)S(1)}, f32[1,256]{1,0:T(1,128)S(1)}, u32[]{:S(2)}, u32[]{:S(2)}) collective-permute-start(f32[1,256]{1,0:T(1,128)S(1)} %bitcast.212), channel_id=1, source_target_pairs={{0,1},{1,2},{2,3},{4,5},{5,6},{6,7},{8,9},{9,10},{10,11},{12,13},{... | collective-permute-start | bytes 3080 | tf_op jit(solution)/shard_map/ppermute | solution.py:19
  191.1 4.7 %collective-permute-start.29 = (f32[1024]{0:T(1024)S(1)}, f32[1024]{0:T(1024)S(1)}, u32[]{:S(2)}, u32[]{:S(2)}) collective-permute-start(f32[1024]{0:T(1024)S(1)} %bitcast.190), channel_id=1, source_target_pairs={{4,0},{8,4},{12,8},{16,12},{20,16},{24,20},{28,24},{0,28},{5,1},{9... | collective-permute-start | bytes 12296 | tf_op jit(solution)/shard_map/ppermute | solution.py:28
  195.8 1.7 fusion.87
  197.8 4.5 %gather_fusion.8 = f32[1024]{0:T(1024)S(1)} fusion(f32[1024]{0:T(1024)S(1)} %broadcast_select_fusion, s32[1024]{0:T(1024)S(1)} %fusion.82), kind=kCustom, calls=%fused_computation.8.clone | custom fusion | bytes 12288 | tf_op jit(solution)/shard_map/jit(_take)/gather | solution.py:121
  202.4 4.8 %fusion.57 = f32[256,1024]{1,0:T(8,128)S(1)} fusion(f32[256,1024]{1,0:T(8,128)S(1)} %copy-done, f32[255,1024]{1,0:T(8,128)} %get-tuple-element.290, f32[1,1024]{1,0:T(1,128)S(1)} %bitcast.173, f32[1,1024]{1,0:T(1,128)S(1)} %bitcast.172, f32[255,1024]{1,0:T(8,128)} %get-tuple-element.289, f32[256,1023]{1,0:T(8,128)} %get-tuple-element.288, ...), kind=kLoop, calls=%fused_computation.114 | loop fusion | flops 3670016 | bytes 12582912 | tf_op jit(solution)/shard_map/add | solution.py:40
  209.5 22.4 %while.13 = (s32[]{:T(128)}, f32[4,256,128]{2,1,0:T(8,128)}, f32[1024]{0:T(1024)S(1)}, f32[1,1024]{1,0:T(1,128)S(1)}, f32[]{:T(128)}, /*index=5*/f32[1024]{0:T(1...) while((s32[]{:T(128)}, f32[4,256,128]{2,1,0:T(8,128)}, ...), condition=%wide.region_1.3_spmd, body=%wide.region_0.2_spmd.sunk | while | flops 141568512 | bytes 2851517 | solution.py:149
  210.7 1.8 gather_fusion
  216.3 1.8 gather_fusion
  221.9 1.8 gather_fusion
  227.5 1.8 gather_fusion
  232.0 25.8 %reduce-scatter.2.cloned.1.call-done = f32[256,128]{1,0:T(8,128)} async-done(((f32[1024,128]{1,0:T(8,128)}), f32[256,128]{1,0:T(8,128)}) %reduce-scatter.2.cloned.1.call-update) | async-done | bytes 131088 | tf_op jit(solution)/shard_map/reduce_scatter | solution.py:152
  258.0 42.2 %all-gather.3.cloned.1.call-done = f32[2048,128]{1,0:T(8,128)} async-done(((f32[256,128]{1,0:T(8,128)}), f32[2048,128]{1,0:T(8,128)}) %all-gather.3.cloned.1.call-update) | async-done | bytes 1048592 | tf_op jit(solution)/shard_map/all_gather | solution.py:158
  301.7 5.8 %psum.7 = f32[16,128]{1,0:T(8,128)S(1)} all-reduce(f32[16,128]{1,0:T(8,128)S(1)} %fusion.66), channel_id=1, replica_groups=mesh['pass'=8,'cell'=4] {'cell'}, use_global_device_ids=true, to_apply=%region_4.6 | all-reduce | flops 2048 | bytes 16384 | tf_op jit(solution)/shard_map/psum | solution.py:166
  (214 shorter events, 30.3 us)
Async XLA Ops:
  7.2 18.1 %copy-start.4 = (f32[256,1024]{1,0:T(8,128)S(1)}, f32[256,1024]{1,0:T(8,128)}, u32[]{:S(2)}) copy-start(f32[256,1024]{1,0:T(8,128)} %param.18) | copy-start | bytes 3145732
  7.2 250.6 %reduce-scatter.2.cloned.1.call-start = ((), (), s32[]{:S(2)}) async-start(), calls=%async_computation.1 | async-start | bytes 655360 | tf_op jit(solution)/shard_map/reduce_scatter | solution.py:152
  8.5 19.9 %collective-permute-start.2 = (f32[1,256]{1,0:T(1,128)S(1)}, f32[1,256]{1,0:T(1,128)S(1)}, u32[]{:S(2)}, u32[]{:S(2)}) collective-permute-start(f32[1,256]{1,0:T(1,128)S(1)} %bitcast.204), channel_id=1, source_target_pairs={{0,1},{1,2},{2,3},{4,5},{5,6},{6,7},{8,9},{9,10},{10,11},{12,13},{... | collective-permute-start | bytes 3080 | tf_op jit(solution)/shard_map/ppermute | solution.py:19
  10.9 17.4 %collective-permute-start.3 = (f32[1,256]{1,0:T(1,128)S(1)}, f32[1,256]{1,0:T(1,128)S(1)}, u32[]{:S(2)}, u32[]{:S(2)}) collective-permute-start(f32[1,256]{1,0:T(1,128)S(1)} %bitcast.205), channel_id=1, source_target_pairs={{1,0},{2,1},{3,2},{5,4},{6,5},{7,6},{9,8},{10,9},{11,10},{13,12},{... | collective-permute-start | bytes 3080 | tf_op jit(solution)/shard_map/ppermute | solution.py:20
  16.5 12.0 %collective-permute-start = (f32[1024]{0:T(1024)S(1)}, f32[1024]{0:T(1024)S(1)}, u32[]{:S(2)}, u32[]{:S(2)}) collective-permute-start(f32[1024]{0:T(1024)S(1)} %bitcast.188), channel_id=1, source_target_pairs={{28,0},{0,4},{4,8},{8,12},{12,16},{16,20},{20,24},{24,28},{29,1},{... | collective-permute-start | bytes 12296 | tf_op jit(solution)/shard_map/ppermute | solution.py:28
  18.9 9.7 %collective-permute-start.1 = (f32[1024]{0:T(1024)S(1)}, f32[1024]{0:T(1024)S(1)}, u32[]{:S(2)}, u32[]{:S(2)}) collective-permute-start(f32[1024]{0:T(1024)S(1)} %bitcast.187), channel_id=1, source_target_pairs={{4,0},{8,4},{12,8},{16,12},{20,16},{24,20},{28,24},{0,28},{5,1},{9... | collective-permute-start | bytes 12296 | tf_op jit(solution)/shard_map/ppermute | solution.py:28
  22.0 4.9 %copy-start.10 = (s32[1,1024]{1,0:T(1,128)S(1)}, s32[1,1024]{1,0:T(1,128)}, u32[]{:S(2)}) copy-start(s32[1,1024]{1,0:T(1,128)} %param.23) | copy-start | bytes 12292
  22.0 5.0 %copy-start.11 = (f32[2,1024]{1,0:T(2,128)S(1)}, f32[2,1024]{1,0:T(2,128)}, u32[]{:S(2)}) copy-start(f32[2,1024]{1,0:T(2,128)} %param.28) | copy-start | bytes 24580
  22.0 5.1 %copy-start.12 = (f32[2,1024]{1,0:T(2,128)S(1)}, f32[2,1024]{1,0:T(2,128)}, u32[]{:S(2)}) copy-start(f32[2,1024]{1,0:T(2,128)} %param.27) | copy-start | bytes 24580
  22.0 5.1 %copy-start.13 = (f32[2,1024]{1,0:T(2,128)S(1)}, f32[2,1024]{1,0:T(2,128)}, u32[]{:S(2)}) copy-start(f32[2,1024]{1,0:T(2,128)} %param.25) | copy-start | bytes 24580
  22.0 5.2 %copy-start.14 = (f32[2,1024]{1,0:T(2,128)S(1)}, f32[2,1024]{1,0:T(2,128)}, u32[]{:S(2)}) copy-start(f32[2,1024]{1,0:T(2,128)} %param.26) | copy-start | bytes 24580
  22.0 5.2 %copy-start.15 = (f32[2,1024]{1,0:T(2,128)S(1)}, f32[2,1024]{1,0:T(2,128)}, u32[]{:S(2)}) copy-start(f32[2,1024]{1,0:T(2,128)} %param.29) | copy-start | bytes 24580
  22.0 5.2 %copy-start.8 = (f32[3,1024]{1,0:T(4,128)S(1)}, f32[3,1024]{1,0:T(4,128)}, u32[]{:S(2)}) copy-start(f32[3,1024]{1,0:T(4,128)} %param.30) | copy-start | bytes 36868
  25.3 7.9 %copy-start = (f32[256,1024]{1,0:T(8,128)S(1)}, f32[256,1024]{1,0:T(8,128)}, u32[]{:S(2)}) copy-start(f32[256,1024]{1,0:T(8,128)} %param.20) | copy-start | bytes 3145732
  38.2 7.1 %copy-start.7 = (f32[1,8,1024]{2,1,0:T(8,128)S(1)}, f32[1,8,1024]{2,1,0:T(8,128)}, u32[]{:S(2)}) copy-start(f32[1,8,1024]{2,1,0:T(8,128)} %param.21) | copy-start | bytes 98308
  39.9 12.1 %collective-permute-start.6 = (f32[1,256]{1,0:T(1,128)S(1)}, f32[1,256]{1,0:T(1,128)S(1)}, u32[]{:S(2)}, u32[]{:S(2)}) collective-permute-start(f32[1,256]{1,0:T(1,128)S(1)} %bitcast.208), channel_id=1, source_target_pairs={{0,1},{1,2},{2,3},{4,5},{5,6},{6,7},{8,9},{9,10},{10,11},{12,13},{... | collective-permute-start | bytes 3080 | tf_op jit(solution)/shard_map/ppermute | solution.py:19
  43.9 7.9 %collective-permute-start.7 = (f32[1,256]{1,0:T(1,128)S(1)}, f32[1,256]{1,0:T(1,128)S(1)}, u32[]{:S(2)}, u32[]{:S(2)}) collective-permute-start(f32[1,256]{1,0:T(1,128)S(1)} %bitcast.213), channel_id=1, source_target_pairs={{1,0},{2,1},{3,2},{5,4},{6,5},{7,6},{9,8},{10,9},{11,10},{13,12},{... | collective-permute-start | bytes 3080 | tf_op jit(solution)/shard_map/ppermute | solution.py:20
  45.3 6.8 %collective-permute-start.4 = (f32[1024]{0:T(1024)S(1)}, f32[1024]{0:T(1024)S(1)}, u32[]{:S(2)}, u32[]{:S(2)}) collective-permute-start(f32[1024]{0:T(1024)S(1)} %bitcast.194), channel_id=1, source_target_pairs={{28,0},{0,4},{4,8},{8,12},{12,16},{16,20},{20,24},{24,28},{29,1},{... | collective-permute-start | bytes 12296 | tf_op jit(solution)/shard_map/ppermute | solution.py:28
  45.4 6.7 %collective-permute-start.5 = (f32[1024]{0:T(1024)S(1)}, f32[1024]{0:T(1024)S(1)}, u32[]{:S(2)}, u32[]{:S(2)}) collective-permute-start(f32[1024]{0:T(1024)S(1)} %bitcast.191), channel_id=1, source_target_pairs={{4,0},{8,4},{12,8},{16,12},{20,16},{24,20},{28,24},{0,28},{5,1},{9... | collective-permute-start | bytes 12296 | tf_op jit(solution)/shard_map/ppermute | solution.py:28
  61.5 13.7 %copy-start.1 = (f32[256,1024]{1,0:T(8,128)}, f32[256,1024]{1,0:T(8,128)S(1)}, u32[]{:S(2)}) copy-start(f32[256,1024]{1,0:T(8,128)S(1)} %fusion.27) | copy-start | bytes 3145732
  63.2 12.1 %collective-permute-start.10 = (f32[1,256]{1,0:T(1,128)S(1)}, f32[1,256]{1,0:T(1,128)S(1)}, u32[]{:S(2)}, u32[]{:S(2)}) collective-permute-start(f32[1,256]{1,0:T(1,128)S(1)} %bitcast.218), channel_id=1, source_target_pairs={{0,1},{1,2},{2,3},{4,5},{5,6},{6,7},{8,9},{9,10},{10,11},{12,13},{... | collective-permute-start | bytes 3080 | tf_op jit(solution)/shard_map/ppermute | solution.py:19
  67.3 7.9 %collective-permute-start.11 = (f32[1,256]{1,0:T(1,128)S(1)}, f32[1,256]{1,0:T(1,128)S(1)}, u32[]{:S(2)}, u32[]{:S(2)}) collective-permute-start(f32[1,256]{1,0:T(1,128)S(1)} %bitcast.224), channel_id=1, source_target_pairs={{1,0},{2,1},{3,2},{5,4},{6,5},{7,6},{9,8},{10,9},{11,10},{13,12},{... | collective-permute-start | bytes 3080 | tf_op jit(solution)/shard_map/ppermute | solution.py:20
  68.6 6.8 %collective-permute-start.8 = (f32[1024]{0:T(1024)S(1)}, f32[1024]{0:T(1024)S(1)}, u32[]{:S(2)}, u32[]{:S(2)}) collective-permute-start(f32[1024]{0:T(1024)S(1)} %bitcast.197), channel_id=1, source_target_pairs={{28,0},{0,4},{4,8},{8,12},{12,16},{16,20},{20,24},{24,28},{29,1},{... | collective-permute-start | bytes 12296 | tf_op jit(solution)/shard_map/ppermute | solution.py:28
  68.7 6.7 %collective-permute-start.9 = (f32[1024]{0:T(1024)S(1)}, f32[1024]{0:T(1024)S(1)}, u32[]{:S(2)}, u32[]{:S(2)}) collective-permute-start(f32[1024]{0:T(1024)S(1)} %bitcast.200), channel_id=1, source_target_pairs={{4,0},{8,4},{12,8},{16,12},{20,16},{24,20},{28,24},{0,28},{5,1},{9... | collective-permute-start | bytes 12296 | tf_op jit(solution)/shard_map/ppermute | solution.py:28
  86.8 12.3 %collective-permute-start.14 = (f32[1,256]{1,0:T(1,128)S(1)}, f32[1,256]{1,0:T(1,128)S(1)}, u32[]{:S(2)}, u32[]{:S(2)}) collective-permute-start(f32[1,256]{1,0:T(1,128)S(1)} %bitcast.207), channel_id=1, source_target_pairs={{0,1},{1,2},{2,3},{4,5},{5,6},{6,7},{8,9},{9,10},{10,11},{12,13},{... | collective-permute-start | bytes 3080 | tf_op jit(solution)/shard_map/ppermute | solution.py:19
  91.1 7.9 %collective-permute-start.15 = (f32[1,256]{1,0:T(1,128)S(1)}, f32[1,256]{1,0:T(1,128)S(1)}, u32[]{:S(2)}, u32[]{:S(2)}) collective-permute-start(f32[1,256]{1,0:T(1,128)S(1)} %bitcast.210), channel_id=1, source_target_pairs={{1,0},{2,1},{3,2},{5,4},{6,5},{7,6},{9,8},{10,9},{11,10},{13,12},{... | collective-permute-start | bytes 3080 | tf_op jit(solution)/shard_map/ppermute | solution.py:20
  92.5 6.8 %collective-permute-start.12 = (f32[1024]{0:T(1024)S(1)}, f32[1024]{0:T(1024)S(1)}, u32[]{:S(2)}, u32[]{:S(2)}) collective-permute-start(f32[1024]{0:T(1024)S(1)} %bitcast.195), channel_id=1, source_target_pairs={{28,0},{0,4},{4,8},{8,12},{12,16},{16,20},{20,24},{24,28},{29,1},{... | collective-permute-start | bytes 12296 | tf_op jit(solution)/shard_map/ppermute | solution.py:28
  92.6 6.7 %collective-permute-start.13 = (f32[1024]{0:T(1024)S(1)}, f32[1024]{0:T(1024)S(1)}, u32[]{:S(2)}, u32[]{:S(2)}) collective-permute-start(f32[1024]{0:T(1024)S(1)} %bitcast.192), channel_id=1, source_target_pairs={{4,0},{8,4},{12,8},{16,12},{20,16},{24,20},{28,24},{0,28},{5,1},{9... | collective-permute-start | bytes 12296 | tf_op jit(solution)/shard_map/ppermute | solution.py:28
  108.6 13.9 %copy-start.2 = (f32[256,1024]{1,0:T(8,128)}, f32[256,1024]{1,0:T(8,128)S(1)}, u32[]{:S(2)}) copy-start(f32[256,1024]{1,0:T(8,128)S(1)} %fusion.37) | copy-start | bytes 3145732
  110.4 12.4 %collective-permute-start.18 = (f32[1,256]{1,0:T(1,128)S(1)}, f32[1,256]{1,0:T(1,128)S(1)}, u32[]{:S(2)}, u32[]{:S(2)}) collective-permute-start(f32[1,256]{1,0:T(1,128)S(1)} %bitcast.219), channel_id=1, source_target_pairs={{0,1},{1,2},{2,3},{4,5},{5,6},{6,7},{8,9},{9,10},{10,11},{12,13},{... | collective-permute-start | bytes 3080 | tf_op jit(solution)/shard_map/ppermute | solution.py:19
  114.7 7.9 %collective-permute-start.19 = (f32[1,256]{1,0:T(1,128)S(1)}, f32[1,256]{1,0:T(1,128)S(1)}, u32[]{:S(2)}, u32[]{:S(2)}) collective-permute-start(f32[1,256]{1,0:T(1,128)S(1)} %bitcast.226), channel_id=1, source_target_pairs={{1,0},{2,1},{3,2},{5,4},{6,5},{7,6},{9,8},{10,9},{11,10},{13,12},{... | collective-permute-start | bytes 3080 | tf_op jit(solution)/shard_map/ppermute | solution.py:20
  116.1 6.8 %collective-permute-start.16 = (f32[1024]{0:T(1024)S(1)}, f32[1024]{0:T(1024)S(1)}, u32[]{:S(2)}, u32[]{:S(2)}) collective-permute-start(f32[1024]{0:T(1024)S(1)} %bitcast.198), channel_id=1, source_target_pairs={{28,0},{0,4},{4,8},{8,12},{12,16},{16,20},{20,24},{24,28},{29,1},{... | collective-permute-start | bytes 12296 | tf_op jit(solution)/shard_map/ppermute | solution.py:28
  116.2 6.7 %collective-permute-start.17 = (f32[1024]{0:T(1024)S(1)}, f32[1024]{0:T(1024)S(1)}, u32[]{:S(2)}, u32[]{:S(2)}) collective-permute-start(f32[1024]{0:T(1024)S(1)} %bitcast.201), channel_id=1, source_target_pairs={{4,0},{8,4},{12,8},{16,12},{20,16},{24,20},{28,24},{0,28},{5,1},{9... | collective-permute-start | bytes 12296 | tf_op jit(solution)/shard_map/ppermute | solution.py:28
  134.3 11.0 %collective-permute-start.22 = (f32[1,256]{1,0:T(1,128)S(1)}, f32[1,256]{1,0:T(1,128)S(1)}, u32[]{:S(2)}, u32[]{:S(2)}) collective-permute-start(f32[1,256]{1,0:T(1,128)S(1)} %bitcast.209), channel_id=1, source_target_pairs={{0,1},{1,2},{2,3},{4,5},{5,6},{6,7},{8,9},{9,10},{10,11},{12,13},{... | collective-permute-start | bytes 3080 | tf_op jit(solution)/shard_map/ppermute | solution.py:19
  138.4 6.6 %collective-permute-start.23 = (f32[1,256]{1,0:T(1,128)S(1)}, f32[1,256]{1,0:T(1,128)S(1)}, u32[]{:S(2)}, u32[]{:S(2)}) collective-permute-start(f32[1,256]{1,0:T(1,128)S(1)} %bitcast.215), channel_id=1, source_target_pairs={{1,0},{2,1},{3,2},{5,4},{6,5},{7,6},{9,8},{10,9},{11,10},{13,12},{... | collective-permute-start | bytes 3080 | tf_op jit(solution)/shard_map/ppermute | solution.py:20
  139.8 5.6 %collective-permute-start.21 = (f32[1024]{0:T(1024)S(1)}, f32[1024]{0:T(1024)S(1)}, u32[]{:S(2)}, u32[]{:S(2)}) collective-permute-start(f32[1024]{0:T(1024)S(1)} %bitcast.193), channel_id=1, source_target_pairs={{4,0},{8,4},{12,8},{16,12},{20,16},{24,20},{28,24},{0,28},{5,1},{9... | collective-permute-start | bytes 12296 | tf_op jit(solution)/shard_map/ppermute | solution.py:28
  143.3 6.4 %collective-permute-start.20 = (f32[1024]{0:T(1024)S(1)}, f32[1024]{0:T(1024)S(1)}, u32[]{:S(2)}, u32[]{:S(2)}) collective-permute-start(f32[1024]{0:T(1024)S(1)} %bitcast.196), channel_id=1, source_target_pairs={{28,0},{0,4},{4,8},{8,12},{12,16},{16,20},{20,24},{24,28},{29,1},{... | collective-permute-start | bytes 12296 | tf_op jit(solution)/shard_map/ppermute | solution.py:28
  159.0 13.8 %copy-start.3 = (f32[256,1024]{1,0:T(8,128)}, f32[256,1024]{1,0:T(8,128)S(1)}, u32[]{:S(2)}) copy-start(f32[256,1024]{1,0:T(8,128)S(1)} %fusion.47) | copy-start | bytes 3145732
  160.7 12.3 %collective-permute-start.26 = (f32[1,256]{1,0:T(1,128)S(1)}, f32[1,256]{1,0:T(1,128)S(1)}, u32[]{:S(2)}, u32[]{:S(2)}) collective-permute-start(f32[1,256]{1,0:T(1,128)S(1)} %bitcast.220), channel_id=1, source_target_pairs={{0,1},{1,2},{2,3},{4,5},{5,6},{6,7},{8,9},{9,10},{10,11},{12,13},{... | collective-permute-start | bytes 3080 | tf_op jit(solution)/shard_map/ppermute | solution.py:19
  165.0 7.9 %collective-permute-start.27 = (f32[1,256]{1,0:T(1,128)S(1)}, f32[1,256]{1,0:T(1,128)S(1)}, u32[]{:S(2)}, u32[]{:S(2)}) collective-permute-start(f32[1,256]{1,0:T(1,128)S(1)} %bitcast.228), channel_id=1, source_target_pairs={{1,0},{2,1},{3,2},{5,4},{6,5},{7,6},{9,8},{10,9},{11,10},{13,12},{... | collective-permute-start | bytes 3080 | tf_op jit(solution)/shard_map/ppermute | solution.py:20
  166.3 6.8 %collective-permute-start.24 = (f32[1024]{0:T(1024)S(1)}, f32[1024]{0:T(1024)S(1)}, u32[]{:S(2)}, u32[]{:S(2)}) collective-permute-start(f32[1024]{0:T(1024)S(1)} %bitcast.199), channel_id=1, source_target_pairs={{28,0},{0,4},{4,8},{8,12},{12,16},{16,20},{20,24},{24,28},{29,1},{... | collective-permute-start | bytes 12296 | tf_op jit(solution)/shard_map/ppermute | solution.py:28
  166.4 6.7 %collective-permute-start.25 = (f32[1024]{0:T(1024)S(1)}, f32[1024]{0:T(1024)S(1)}, u32[]{:S(2)}, u32[]{:S(2)}) collective-permute-start(f32[1024]{0:T(1024)S(1)} %bitcast.202), channel_id=1, source_target_pairs={{4,0},{8,4},{12,8},{16,12},{20,16},{24,20},{28,24},{0,28},{5,1},{9... | collective-permute-start | bytes 12296 | tf_op jit(solution)/shard_map/ppermute | solution.py:28
  184.6 13.0 %collective-permute-start.30 = (f32[1,256]{1,0:T(1,128)S(1)}, f32[1,256]{1,0:T(1,128)S(1)}, u32[]{:S(2)}, u32[]{:S(2)}) collective-permute-start(f32[1,256]{1,0:T(1,128)S(1)} %bitcast.212), channel_id=1, source_target_pairs={{0,1},{1,2},{2,3},{4,5},{5,6},{6,7},{8,9},{9,10},{10,11},{12,13},{... | collective-permute-start | bytes 3080 | tf_op jit(solution)/shard_map/ppermute | solution.py:19
  189.8 7.8 %collective-permute-start.31 = (f32[1,256]{1,0:T(1,128)S(1)}, f32[1,256]{1,0:T(1,128)S(1)}, u32[]{:S(2)}, u32[]{:S(2)}) collective-permute-start(f32[1,256]{1,0:T(1,128)S(1)} %bitcast.217), channel_id=1, source_target_pairs={{1,0},{2,1},{3,2},{5,4},{6,5},{7,6},{9,8},{10,9},{11,10},{13,12},{... | collective-permute-start | bytes 3080 | tf_op jit(solution)/shard_map/ppermute | solution.py:20
  191.1 6.8 %collective-permute-start.28 = (f32[1024]{0:T(1024)S(1)}, f32[1024]{0:T(1024)S(1)}, u32[]{:S(2)}, u32[]{:S(2)}) collective-permute-start(f32[1024]{0:T(1024)S(1)} %bitcast.189), channel_id=1, source_target_pairs={{28,0},{0,4},{4,8},{8,12},{12,16},{16,20},{20,24},{24,28},{29,1},{... | collective-permute-start | bytes 12296 | tf_op jit(solution)/shard_map/ppermute | solution.py:28
  191.1 6.7 %collective-permute-start.29 = (f32[1024]{0:T(1024)S(1)}, f32[1024]{0:T(1024)S(1)}, u32[]{:S(2)}, u32[]{:S(2)}) collective-permute-start(f32[1024]{0:T(1024)S(1)} %bitcast.190), channel_id=1, source_target_pairs={{4,0},{8,4},{12,8},{16,12},{20,16},{24,20},{28,24},{0,28},{5,1},{9... | collective-permute-start | bytes 12296 | tf_op jit(solution)/shard_map/ppermute | solution.py:28
  207.2 1.0 copy-start.5
  209.5 48.4 %copy-start.9 = (s32[1024]{0:T(1024)S(1)}, s32[1024]{0:T(1024)}, u32[]{:S(2)}) copy-start(s32[1024]{0:T(1024)} %param.31) | copy-start | bytes 12292
  231.9 68.3 %all-gather.3.cloned.1.call-start = ((), (), s32[]{:S(2)}) async-start(), calls=%async_computation.2 | async-start | bytes 1179648 | tf_op jit(solution)/shard_map/all_gather | solution.py:158
  301.5 6.6 %copy-start.6 = (f32[256,128]{1,0:T(8,128)}, f32[256,128]{1,0:T(8,128)S(1)}, u32[]{:S(2)}) copy-start(f32[256,128]{1,0:T(8,128)S(1)} %reduce_sum.18) | copy-start | bytes 393220
Sparse Core Ops, SparseCore 0:
  232.1 25.7 reduce-scatter.1
  259.9 40.2 all-gather.2
